TPU v7x, 32 devices: a whole 2x2x4 slice. The times are simulated.
32 devices in a mesh: blk: 16 (over z, x, core), rep: 2 (over y).
Axes of the slice: x: 2, y: 2, z: 4, core: 2. Of those that a mesh axis runs over, the one named last changes fastest.
Arguments:
- measured: float32 [3, 16, 8, 1536], P(None, 'blk', None, 'rep'), may hold values from -4 to 4
- rot_vector: float32 [3, 16, 8, 1536], P(None, 'blk', None, 'rep'), may hold values from -6 to 6
- confidence: float32 [3, 16, 8, 1536], P(None, 'blk', None, 'rep'), may hold values from 0.5 to 2
- first_local: int32 [16, 8, 1536], P('blk', None, 'rep'), may hold values from 0 to 2047
- second_local: int32 [16, 8, 1536], P('blk', None, 'rep'), may hold values from 0 to 2047
- edge_counts: int32 [16, 8, 2], P('blk', None, 'rep'), may hold values from 256 to 768, as said below
- start_angles: float32 [3, 32768], P(None, 'blk'), may hold values from -4 to 4
- anchor: float32 [32768], P('blk'), may hold values from 0.05 to 0.5
Outputs:
- estimate: float32 [3, 32768], P(None, 'blk')
- weights: float32 [16, 8, 1536], P('blk', None, 'rep')
Inputs may be any that keep to these rules, and one draw needn't show every extreme that they name: `edge_counts`: live edges of a tile pair on one device fill its first slots; in every tile some pair holds 768 live edges on one device.
All inputs are finite; a program needn't handle non-finite values.
Results may differ from a plain program's by a relative error of at most 0.0001.
Values sent between devices are 32-bit elements; how exact they have to be, the bound alone decides.
No kernel may reach another device: no remote copies, remote signals or barrier semaphores. Data moves between devices by JAX's collectives and lax.ppermute only.
A program may use at most 128 MiB of HBM per device.

v0:
```python
import jax
import jax.numpy as jnp
from jax import lax
from jax.sharding import PartitionSpec as P

PASSES = 2
ITERS = 2


PAIRS = ((0, 0), (0, 1), (0, 2), (1, 1), (1, 2), (2, 2))
LOOKUP = ((0, 1, 2), (1, 3, 4), (2, 4, 5))
SOFTEN = 0.05


def shifted(value, axis, steps):
    count = lax.axis_size(axis)
    pairs = [(source, (source + steps) % count) for source in range(count)]
    return lax.ppermute(value, axis, pairs)


def rotations(vector):
    squared = vector[0] * vector[0] + vector[1] * vector[1] + vector[2] * vector[2]
    factor = 2.0 / (1.0 + squared)
    zeros = jnp.zeros_like(squared)
    skewed = (
        (zeros, -vector[2], vector[1]),
        (vector[2], zeros, -vector[0]),
        (-vector[1], vector[0], zeros),
    )
    matrix_rows = []
    for first in range(3):
        entries = []
        for second in range(3):
            term = skewed[first][second] + vector[first] * vector[second]
            if first == second:
                entries.append(1.0 + factor * (term - squared))
            else:
                entries.append(factor * term)
        matrix_rows.append(jnp.stack(entries))
    return jnp.stack(matrix_rows)


def rotate(rotation, vector):
    return jnp.sum(rotation * vector[None], axis=1)


def rotate_back(rotation, vector):
    return jnp.sum(rotation * vector[:, None], axis=0)


def block_parts(weighted, rotation):
    far_list = []
    near_list = []
    for first, second in PAIRS:
        near_list.append(jnp.sum(rotation[:, first] * weighted * rotation[:, second], axis=0))
        if first == second:
            far_list.append(weighted[first])
        else:
            far_list.append(jnp.zeros_like(weighted[0]))
    return (jnp.stack(far_list), jnp.stack(near_list))


def inverse_apply(blocks, vector):
    adjugate = jnp.stack(
        [
            blocks[3] * blocks[5] - blocks[4] * blocks[4],
            blocks[2] * blocks[4] - blocks[1] * blocks[5],
            blocks[1] * blocks[4] - blocks[2] * blocks[3],
            blocks[0] * blocks[5] - blocks[2] * blocks[2],
            blocks[1] * blocks[2] - blocks[0] * blocks[4],
            blocks[0] * blocks[3] - blocks[1] * blocks[1],
        ]
    )
    determinant = blocks[0] * adjugate[0] + blocks[1] * adjugate[1] + blocks[2] * adjugate[2]
    result = []
    for first in range(3):
        total = (
            adjugate[LOOKUP[first][0]] * vector[0]
            + adjugate[LOOKUP[first][1]] * vector[1]
            + adjugate[LOOKUP[first][2]] * vector[2]
        )
        result.append(total / determinant)
    return jnp.stack(result)


def spread(terms, index, total):
    return jax.vmap(lambda values: jax.ops.segment_sum(values, index, num_segments=total))(terms)


def on_device(
    measured, rot_vector, confidence, first_local, second_local, edge_counts, start_angles, anchor
):
    tile_cams = start_angles.shape[1]
    pair_count = first_local.shape[1]
    slot_count = first_local.shape[2]
    window_span = pair_count * tile_cams
    first = first_local.reshape(-1)
    second = (
        jnp.arange(pair_count, dtype=jnp.int32)[:, None] * tile_cams + second_local[0]
    ).reshape(-1)
    live = (
        (jnp.arange(slot_count, dtype=jnp.int32)[None, :] < edge_counts[0])
        .astype(jnp.float32)
        .reshape(-1)
    )
    measured = measured.reshape(3, -1)
    confidence = confidence.reshape(3, -1)
    rotation = rotations(rot_vector.reshape(3, -1))
    diagonal = jnp.stack(
        [anchor if first_c == second_c else jnp.zeros_like(anchor) for first_c, second_c in PAIRS]
    )

    def window_of(field):
        window = field
        width = 1
        while width < pair_count:
            ahead = shifted(window, "blk", -width)
            window = jnp.concatenate([window, ahead], axis=1)
            width = width * 2
        return window

    def returned(far_sums):
        current = far_sums
        width = pair_count
        while width > 1:
            half_width = width // 2
            moved = shifted(current[:, half_width:width], "blk", half_width)
            current = current[:, :half_width] + moved
            width = half_width
        return current[:, 0]

    def reduce_halves(sums):
        return lax.psum(sums, "rep")

    def collect(far_terms, near_terms):
        channels = far_terms.shape[0]
        far_sums = spread(far_terms, second, window_span).reshape(channels, pair_count, tile_cams)
        near_sums = spread(near_terms, first, tile_cams)
        return reduce_halves(returned(far_sums) + near_sums)

    def precond_sum(residual, scaled):
        return lax.psum(jnp.sum(residual * scaled), "blk")

    estimate = start_angles
    weights = live
    for sweep_index in range(PASSES):
        window = window_of(estimate)
        misfit = measured - (window[:, second] - rotate(rotation, estimate[:, first]))
        weights = live / jnp.sqrt(jnp.sum(confidence * misfit * misfit, axis=0) + SOFTEN * SOFTEN)
        weighted = weights * confidence
        terms = weighted * misfit
        far_part, near_part = block_parts(weighted, rotation)
        near_terms = jnp.concatenate([-rotate_back(rotation, terms), near_part], axis=0)
        far_terms = jnp.concatenate([terms, far_part], axis=0)
        totals = collect(far_terms, near_terms)
        residual = totals[:3] - anchor * estimate
        blocks = totals[3:] + diagonal
        scaled = inverse_apply(blocks, residual)
        direction = scaled
        norm_now = precond_sum(residual, scaled)
        for inner_index in range(ITERS):
            window = window_of(direction)
            changed = window[:, second] - rotate(rotation, direction[:, first])
            pushed = weighted * changed
            image = collect(pushed, -rotate_back(rotation, pushed)) + anchor * direction
            step_size = norm_now / lax.psum(jnp.sum(direction * image), "blk")
            estimate = estimate + step_size * direction
            residual = residual - step_size * image
            if inner_index + 1 < ITERS:
                scaled = inverse_apply(blocks, residual)
                norm_next = precond_sum(residual, scaled)
                direction = scaled + norm_next / norm_now * direction
                norm_now = norm_next
    return (estimate, weights.reshape(1, pair_count, slot_count))


def solution(mesh):
    return jax.shard_map(
        on_device,
        mesh=mesh,
        in_specs=(
            P(None, "blk", None, "rep"),
            P(None, "blk", None, "rep"),
            P(None, "blk", None, "rep"),
            P("blk", None, "rep"),
            P("blk", None, "rep"),
            P("blk", None, "rep"),
            P(None, "blk"),
            P("blk"),
        ),
        out_specs=(P(None, "blk"), P("blk", None, "rep")),
        check_vma=False,
    )
```

profile of v0, /device:TPU:0, one launch (start us, length us, event | category | flops | bytes accessed | tf_op | source)
XLA Modules:
  0.0 1505.5 jit_solution(13354158175996071067)
XLA Ops:
  16.6 17.3 %gather_fusion.1 = f32[6144,3]{1,0:T(8,128)S(1)} fusion(f32[3,2048]{0,1:T(8,128)} %copy.781, s32[6144]{0:T(1024)S(1)} %broadcast_clamp_fusion), kind=kCustom, calls=%fused_computation.1 | custom fusion | bytes 172032 | tf_op jit(solution)/shard_map/gather | solution.py:148
  64.2 24.3 %gather_fusion = f32[6144,3]{1,0:T(8,128)} fusion(f32[3,16384]{0,1:T(8,128)} %copy.780, s32[6144]{0:T(1024)S(1)} %broadcast_clamp_fusion.1), kind=kCustom, calls=%fused_computation | custom fusion | bytes 172032 | tf_op jit(solution)/shard_map/gather | solution.py:148
  95.9 9.5 fusion.12
  132.0 37.4 %scatter_custom_fusion = f32[9,16384]{0,1:T(8,128)} fusion(s32[6144]{0:T(1024)} %bitcast.235, f32[6144,9]{1,0:T(8,128)} %copy.791, f32[]{:T(128)} %constant.7.clone.1), kind=kCustom, calls=%fused_computation.39 | custom fusion | flops 55296 | bytes 590336 | tf_op jit(solution)/shard_map/vmap()/scatter-add | solution.py:87
  169.4 7.4 fusion.42
  213.9 32.3 %scatter_fusion = f32[9,2048]{0,1:T(8,128)} fusion(f32[9,2048]{0,1:T(8,128)} %bitcast.191, s32[6144]{0:T(1024)S(1)} %reshape.813, f32[6144,9]{1,0:T(8,128)} %copy.799), kind=kCustom, calls=%fused_computation.13 | custom fusion | flops 55296 | bytes 688128 | tf_op jit(solution)/shard_map/vmap()/scatter-add | solution.py:87
  251.1 20.2 %all-reduce.5.cloned.1.call-done = f32[9,2048]{1,0:T(8,128)} async-done(((f32[9,2048]{1,0:T(8,128)}), f32[9,2048]{1,0:T(8,128)}) %all-reduce.5.cloned.1.call-update) | async-done | bytes 73744 | tf_op jit(solution)/shard_map/psum | solution.py:133
  283.4 22.1 %gather_fusion.3 = f32[6144,3]{1,0:T(8,128)} fusion(f32[3,2048]{0,1:T(8,128)} %copy.802, s32[6144]{0:T(1024)S(1)} %broadcast_clamp_fusion), kind=kCustom, calls=%fused_computation.3 | custom fusion | bytes 172032 | tf_op jit(solution)/shard_map/gather | solution.py:163
  317.3 5.7 copy.801
  323.0 24.3 %gather_fusion.2 = f32[6144,3]{1,0:T(8,128)} fusion(f32[3,16384]{0,1:T(8,128)} %copy.801, s32[6144]{0:T(1024)S(1)} %broadcast_clamp_fusion.1), kind=kCustom, calls=%fused_computation.2 | custom fusion | bytes 172032 | tf_op jit(solution)/shard_map/gather | solution.py:163
  352.2 34.2 %scatter_custom_fusion.2 = f32[3,16384]{0,1:T(8,128)} fusion(s32[6144]{0:T(1024)} %bitcast.236, f32[]{:T(128)} %constant.7.clone.1, f32[3,6144]{0,1:T(8,128)} %fusion.21), kind=kCustom, calls=%fused_computation.35 | custom fusion | flops 18432 | bytes 3342848 | tf_op jit(solution)/shard_map/vmap()/scatter-add | solution.py:87
  386.4 7.4 fusion.41
  424.1 32.3 %scatter_fusion.1 = f32[3,2048]{0,1:T(8,128)} fusion(f32[3,2048]{0,1:T(8,128)} %bitcast.194, s32[6144]{0:T(1024)S(1)} %reshape.813, f32[6144,3]{1,0:T(8,128)} %copy.809), kind=kCustom, calls=%fused_computation.15 | custom fusion | flops 18432 | bytes 245760 | tf_op jit(solution)/shard_map/vmap()/scatter-add | solution.py:87
  458.6 8.6 psum.100
  468.7 30.2 %all-reduce.1 = (f32[]{:T(128)}, f32[]{:T(128)}) all-reduce(f32[]{:T(128)} %get-tuple-element.31, f32[]{:T(128)} %get-tuple-element.30), channel_id=1, replica_groups=mesh['blk'=16,'rep'=2] {'blk'}, use_global_device_ids=true, to_apply=%region_13.0 | all-reduce | flops 2 | bytes 16 | tf_op jit(solution)/shard_map/psum | solution.py:142
  504.1 30.1 %psum.102 = f32[]{:T(128)} all-reduce(f32[]{:T(128)} %multiply_reduce_fusion.17), channel_id=1, replica_groups=mesh['blk'=16,'rep'=2] {'blk'}, use_global_device_ids=true, to_apply=%region_22.0 | all-reduce | flops 1 | bytes 8 | tf_op jit(solution)/shard_map/psum | solution.py:142
  540.7 22.1 %gather_fusion.5 = f32[6144,3]{1,0:T(8,128)} fusion(f32[3,2048]{0,1:T(8,128)} %copy.811, s32[6144]{0:T(1024)S(1)} %broadcast_clamp_fusion), kind=kCustom, calls=%fused_computation.5 | custom fusion | bytes 172032 | tf_op jit(solution)/shard_map/gather | solution.py:163
  580.7 8.2 pad_maximum_fusion
  588.8 24.3 %gather_fusion.4 = f32[6144,3]{1,0:T(8,128)} fusion(f32[3,16384]{0,1:T(8,128)} %pad_maximum_fusion, s32[6144]{0:T(1024)S(1)} %broadcast_clamp_fusion.1), kind=kCustom, calls=%fused_computation.4 | custom fusion | bytes 172032 | tf_op jit(solution)/shard_map/gather | solution.py:163
  618.1 34.2 %scatter_custom_fusion.4 = f32[3,16384]{0,1:T(8,128)} fusion(s32[6144]{0:T(1024)} %bitcast.237, f32[]{:T(128)} %constant.7.clone.1, f32[3,6144]{0,1:T(8,128)} %fusion.19), kind=kCustom, calls=%fused_computation.33 | custom fusion | flops 18432 | bytes 3342848 | tf_op jit(solution)/shard_map/vmap()/scatter-add | solution.py:87
  652.3 7.4 fusion.40
  685.2 33.9 %scatter_fusion.2 = f32[3,2048]{0,1:T(8,128)S(1)} fusion(f32[3,2048]{0,1:T(8,128)S(1)} %bitcast.195, s32[6144]{0:T(1024)S(1)} %reshape.813, f32[6144,3]{1,0:T(8,128)} %copy.822), kind=kCustom, calls=%fused_computation.17 | custom fusion | flops 18432 | bytes 245760 | tf_op jit(solution)/shard_map/vmap()/scatter-add | solution.py:87
  719.4 8.3 psum.103
  728.4 30.3 %psum.104 = f32[]{:T(128)} all-reduce(f32[]{:T(128)} %multiply_reduce_fusion.16), channel_id=1, replica_groups=mesh['blk'=16,'rep'=2] {'blk'}, use_global_device_ids=true, to_apply=%region_29.0 | all-reduce | flops 1 | bytes 8 | tf_op jit(solution)/shard_map/psum | solution.py:166
  762.2 20.9 %gather_fusion.7 = f32[6144,3]{1,0:T(8,128)} fusion(f32[3,2048]{0,1:T(8,128)S(1)} %copy.824, s32[6144]{0:T(1024)S(1)} %broadcast_clamp_fusion), kind=kCustom, calls=%fused_computation.7 | custom fusion | bytes 172032 | tf_op jit(solution)/shard_map/gather | solution.py:148
  795.8 8.9 pad_maximum_fusion.1
  804.7 24.3 %gather_fusion.6 = f32[6144,3]{1,0:T(8,128)} fusion(f32[3,16384]{0,1:T(8,128)} %pad_maximum_fusion.1, s32[6144]{0:T(1024)S(1)} %broadcast_clamp_fusion.1), kind=kCustom, calls=%fused_computation.6 | custom fusion | bytes 172032 | tf_op jit(solution)/shard_map/gather | solution.py:148
  837.0 9.7 fusion.13
  872.6 37.2 %scatter_custom_fusion.6 = f32[9,16384]{0,1:T(8,128)} fusion(s32[6144]{0:T(1024)} %bitcast.238, f32[6144,9]{1,0:T(8,128)} %copy.836, f32[]{:T(128)} %constant.7.clone.1), kind=kCustom, calls=%fused_computation.37 | custom fusion | flops 55296 | bytes 590336 | tf_op jit(solution)/shard_map/vmap()/scatter-add | solution.py:87
  909.8 7.4 fusion.39
  953.1 32.3 %scatter_fusion.3 = f32[9,2048]{0,1:T(8,128)} fusion(f32[9,2048]{0,1:T(8,128)} %bitcast.192, s32[6144]{0:T(1024)S(1)} %reshape.813, f32[6144,9]{1,0:T(8,128)} %copy.841), kind=kCustom, calls=%fused_computation.19 | custom fusion | flops 55296 | bytes 688128 | tf_op jit(solution)/shard_map/vmap()/scatter-add | solution.py:87
  987.7 20.7 %all-reduce.7.cloned.1.call-done = f32[9,2048]{1,0:T(8,128)} async-done(((f32[9,2048]{1,0:T(8,128)}), f32[9,2048]{1,0:T(8,128)}) %all-reduce.7.cloned.1.call-update) | async-done | bytes 73744 | tf_op jit(solution)/shard_map/psum | solution.py:133
  1020.4 22.1 %gather_fusion.9 = f32[6144,3]{1,0:T(8,128)} fusion(f32[3,2048]{0,1:T(8,128)} %copy.844, s32[6144]{0:T(1024)S(1)} %broadcast_clamp_fusion), kind=kCustom, calls=%fused_computation.9 | custom fusion | bytes 172032 | tf_op jit(solution)/shard_map/gather | solution.py:163
  1059.7 24.3 %gather_fusion.8 = f32[6144,3]{1,0:T(8,128)} fusion(f32[3,16384]{0,1:T(8,128)} %copy.843, s32[6144]{0:T(1024)S(1)} %broadcast_clamp_fusion.1), kind=kCustom, calls=%fused_computation.8 | custom fusion | bytes 172032 | tf_op jit(solution)/shard_map/gather | solution.py:163
  1089.0 34.2 %scatter_custom_fusion.8 = f32[3,16384]{0,1:T(8,128)} fusion(s32[6144]{0:T(1024)} %bitcast.239, f32[]{:T(128)} %constant.7.clone.1, f32[3,6144]{0,1:T(8,128)} %fusion.17), kind=kCustom, calls=%fused_computation.31 | custom fusion | flops 18432 | bytes 3342848 | tf_op jit(solution)/shard_map/vmap()/scatter-add | solution.py:87
  1123.2 7.4 fusion.38
  1160.8 32.3 %scatter_fusion.4 = f32[3,2048]{0,1:T(8,128)} fusion(f32[3,2048]{0,1:T(8,128)} %bitcast.196, s32[6144]{0:T(1024)S(1)} %reshape.813, f32[6144,3]{1,0:T(8,128)} %copy.851), kind=kCustom, calls=%fused_computation.21 | custom fusion | flops 18432 | bytes 245760 | tf_op jit(solution)/shard_map/vmap()/scatter-add | solution.py:87
  1195.3 8.6 psum.107
  1205.4 30.2 %all-reduce = (f32[]{:T(128)}, f32[]{:T(128)}) all-reduce(f32[]{:T(128)} %get-tuple-element.29, f32[]{:T(128)} %get-tuple-element.28), channel_id=1, replica_groups=mesh['blk'=16,'rep'=2] {'blk'}, use_global_device_ids=true, to_apply=%region_43.0 | all-reduce | flops 2 | bytes 16 | tf_op jit(solution)/shard_map/psum | solution.py:142
  1241.0 30.2 %psum.109 = f32[]{:T(128)} all-reduce(f32[]{:T(128)} %multiply_reduce_fusion.13), channel_id=1, replica_groups=mesh['blk'=16,'rep'=2] {'blk'}, use_global_device_ids=true, to_apply=%region_52.0 | all-reduce | flops 1 | bytes 8 | tf_op jit(solution)/shard_map/psum | solution.py:142
  1277.9 22.1 %gather_fusion.11 = f32[6144,3]{1,0:T(8,128)} fusion(f32[3,2048]{0,1:T(8,128)} %copy.853, s32[6144]{0:T(1024)S(1)} %broadcast_clamp_fusion), kind=kCustom, calls=%fused_computation.11 | custom fusion | bytes 172032 | tf_op jit(solution)/shard_map/gather | solution.py:163
  1317.8 8.2 pad_maximum_fusion.2
  1326.0 24.3 %gather_fusion.10 = f32[6144,3]{1,0:T(8,128)} fusion(f32[3,16384]{0,1:T(8,128)} %pad_maximum_fusion.2, s32[6144]{0:T(1024)S(1)} %broadcast_clamp_fusion.1), kind=kCustom, calls=%fused_computation.10 | custom fusion | bytes 172032 | tf_op jit(solution)/shard_map/gather | solution.py:163
  1355.2 34.2 %scatter_custom_fusion.10 = f32[3,16384]{0,1:T(8,128)} fusion(s32[6144]{0:T(1024)} %bitcast.240, f32[]{:T(128)} %constant.7.clone.1, f32[3,6144]{0,1:T(8,128)} %fusion.15), kind=kCustom, calls=%fused_computation.29 | custom fusion | flops 18432 | bytes 3342848 | tf_op jit(solution)/shard_map/vmap()/scatter-add | solution.py:87
  1389.4 7.4 fusion.37
  1422.3 33.9 %scatter_fusion.5 = f32[3,2048]{0,1:T(8,128)S(1)} fusion(f32[3,2048]{0,1:T(8,128)S(1)} %bitcast.193, s32[6144]{0:T(1024)S(1)} %reshape.813, f32[6144,3]{1,0:T(8,128)} %copy.864), kind=kCustom, calls=%fused_computation.23 | custom fusion | flops 18432 | bytes 245760 | tf_op jit(solution)/shard_map/vmap()/scatter-add | solution.py:87
  1456.5 8.3 psum.110
  1466.3 30.1 %psum.111 = f32[]{:T(128)} all-reduce(f32[]{:T(128)} %multiply_reduce_fusion.12), channel_id=1, replica_groups=mesh['blk'=16,'rep'=2] {'blk'}, use_global_device_ids=true, to_apply=%region_59.0 | all-reduce | flops 1 | bytes 8 | tf_op jit(solution)/shard_map/psum | solution.py:166
  (440 shorter events, 451.3 us)
Async XLA Ops:
  7.2 264.2 %all-reduce.5.cloned.1.call-start = ((), (), s32[]{:S(2)}) async-start(), calls=%async_computation | async-start | bytes 262144 | tf_op jit(solution)/shard_map/psum | solution.py:133
  7.2 31.1 %collective-permute-start = (f32[3,2048]{1,0:T(4,128)}, f32[3,2048]{1,0:T(4,128)}, u32[]{:S(2)}, u32[]{:S(2)}) collective-permute-start(f32[3,2048]{1,0:T(4,128)} %param.14), channel_id=1, source_target_pairs={{0,30},{2,0},{4,2},{6,4},{8,6},{10,8},{12,10},{14,12},{16,14},{18,... | collective-permute-start | bytes 73736 | tf_op jit(solution)/shard_map/ppermute | solution.py:18
  39.1 4.3 collective-permute-start.1
  44.3 14.1 collective-permute-start.2
  180.2 9.3 collective-permute-start.3
  191.4 8.2 collective-permute-start.4
  202.0 8.0 collective-permute-start.5
  248.5 759.9 %all-reduce.7.cloned.1.call-start = ((), (), s32[]{:S(2)}) async-start(), calls=%async_computation.1 | async-start | bytes 262144 | tf_op jit(solution)/shard_map/psum | solution.py:133
  274.6 4.8 collective-permute-start.6
  280.1 28.3 %collective-permute-start.7 = (f32[3,4096]{1,0:T(4,128)}, f32[3,4096]{1,0:T(4,128)}, u32[]{:S(2)}, u32[]{:S(2)}) collective-permute-start(f32[3,4096]{1,0:T(4,128)} %pad_maximum_fusion.14), channel_id=1, source_target_pairs={{0,28},{2,30},{4,0},{6,2},{8,4},{10,6},{12,8},{14,10},{16,12},{18,... | collective-permute-start | bytes 147464 | tf_op jit(solution)/shard_map/ppermute | solution.py:18
  310.0 5.7 collective-permute-start.8
  397.3 7.9 collective-permute-start.9
  406.2 6.8 collective-permute-start.10
  414.3 6.3 collective-permute-start.11
  536.3 1.7 collective-permute-start.12
  538.6 27.2 %collective-permute-start.13 = (f32[3,4096]{1,0:T(4,128)}, f32[3,4096]{1,0:T(4,128)}, u32[]{:S(2)}, u32[]{:S(2)}) collective-permute-start(f32[3,4096]{1,0:T(4,128)} %pad_maximum_fusion.15), channel_id=1, source_target_pairs={{0,28},{2,30},{4,0},{6,2},{8,4},{10,6},{12,8},{14,10},{16,12},{18,... | collective-permute-start | bytes 147464 | tf_op jit(solution)/shard_map/ppermute | solution.py:18
  567.3 9.9 collective-permute-start.14
  663.2 7.6 collective-permute-start.15
  671.9 6.8 collective-permute-start.16
  678.8 6.0 collective-permute-start.17
  680.8 47.0 %copy-start.18 = (f32[1,2048]{1,0:T(1,128)S(1)}, f32[1,2048]{1,0:T(1,128)}, u32[]{:S(2)}) copy-start(f32[1,2048]{1,0:T(1,128)} %copy-done.17) | copy-start | bytes 24580
  680.8 47.0 %copy-start.24 = (f32[1,2048]{1,0:T(1,128)S(1)}, f32[1,2048]{1,0:T(1,128)}, u32[]{:S(2)}) copy-start(f32[1,2048]{1,0:T(1,128)} %copy-done.23) | copy-start | bytes 24580
  680.8 47.0 %copy-start.26 = (f32[1,2048]{1,0:T(1,128)S(1)}, f32[1,2048]{1,0:T(1,128)}, u32[]{:S(2)}) copy-start(f32[1,2048]{1,0:T(1,128)} %copy-done.25) | copy-start | bytes 24580
  680.8 47.0 %copy-start.51 = (f32[1,2048]{1,0:T(1,128)S(1)}, f32[1,2048]{1,0:T(1,128)}, u32[]{:S(2)}) copy-start(f32[1,2048]{1,0:T(1,128)} %copy-done.50) | copy-start | bytes 24580
  680.8 47.0 %copy-start.53 = (f32[1,2048]{1,0:T(1,128)S(1)}, f32[1,2048]{1,0:T(1,128)}, u32[]{:S(2)}) copy-start(f32[1,2048]{1,0:T(1,128)} %copy-done.52) | copy-start | bytes 24580
  680.8 47.0 %copy-start.59 = (f32[1,2048]{1,0:T(1,128)S(1)}, f32[1,2048]{1,0:T(1,128)}, u32[]{:S(2)}) copy-start(f32[1,2048]{1,0:T(1,128)} %copy-done.58) | copy-start | bytes 24580
  760.1 1.7 collective-permute-start.18
  761.8 23.7 %collective-permute-start.19 = (f32[3,4096]{1,0:T(4,128)S(1)}, f32[3,4096]{1,0:T(4,128)S(1)}, u32[]{:S(2)}, u32[]{:S(2)}) collective-permute-start(f32[3,4096]{1,0:T(4,128)S(1)} %pad_maximum_fusion.16), channel_id=1, source_target_pairs={{0,28},{2,30},{4,0},{6,2},{8,4},{10,6},{12,8},{14,10},{16,12},{18,... | collective-permute-start | bytes 147464 | tf_op jit(solution)/shard_map/ppermute | solution.py:18
  786.2 6.2 collective-permute-start.20
  920.7 9.3 collective-permute-start.21
  931.2 8.0 collective-permute-start.22
  940.7 8.5 collective-permute-start.23
  953.1 56.2 %copy-start.11 = (f32[3,2048]{1,0:T(4,128)S(1)}, f32[3,2048]{1,0:T(4,128)}, u32[]{:S(2)}) copy-start(f32[3,2048]{1,0:T(4,128)} %copy-done.10) | copy-start | bytes 73732
  1011.6 4.8 collective-permute-start.24
  1017.1 28.3 %collective-permute-start.25 = (f32[3,4096]{1,0:T(4,128)}, f32[3,4096]{1,0:T(4,128)}, u32[]{:S(2)}, u32[]{:S(2)}) collective-permute-start(f32[3,4096]{1,0:T(4,128)} %pad_maximum_fusion.17), channel_id=1, source_target_pairs={{0,28},{2,30},{4,0},{6,2},{8,4},{10,6},{12,8},{14,10},{16,12},{18,... | collective-permute-start | bytes 147464 | tf_op jit(solution)/shard_map/ppermute | solution.py:18
  1047.0 5.4 collective-permute-start.26
  1134.0 7.9 collective-permute-start.27
  1142.9 6.8 collective-permute-start.28
  1151.1 6.3 collective-permute-start.29
  1273.4 1.7 collective-permute-start.30
  1275.7 27.2 %collective-permute-start.31 = (f32[3,4096]{1,0:T(4,128)}, f32[3,4096]{1,0:T(4,128)}, u32[]{:S(2)}, u32[]{:S(2)}) collective-permute-start(f32[3,4096]{1,0:T(4,128)} %pad_maximum_fusion.18), channel_id=1, source_target_pairs={{0,28},{2,30},{4,0},{6,2},{8,4},{10,6},{12,8},{14,10},{16,12},{18,... | collective-permute-start | bytes 147464 | tf_op jit(solution)/shard_map/ppermute | solution.py:18
  1304.5 9.9 collective-permute-start.32
  1400.4 7.6 collective-permute-start.33
  1409.0 6.8 collective-permute-start.34
  1415.9 6.0 collective-permute-start.35
  1417.9 47.0 %copy-start.16 = (f32[1,2048]{1,0:T(1,128)S(1)}, f32[1,2048]{1,0:T(1,128)}, u32[]{:S(2)}) copy-start(f32[1,2048]{1,0:T(1,128)} %copy-done.15) | copy-start | bytes 24580
  1418.0 47.6 %copy-start.45 = (f32[8,768]{1,0:T(8,128)S(1)}, f32[8,768]{1,0:T(8,128)}, u32[]{:S(2)}) copy-start(f32[8,768]{1,0:T(8,128)} %copy-done.44) | copy-start | bytes 73732
  1418.0 47.6 %copy-start.73 = (s32[1,8,1]{1,2,0:T(1,128)S(1)}, s32[1,8,1]{1,2,0:T(1,128)}, u32[]{:S(2)}) copy-start(s32[1,8,1]{1,2,0:T(1,128)} %param.13) | copy-start | bytes 100
  (64 other events, 584.2 us)
Sparse Core Ops, SparseCore 0:
  248.6 22.7 all-reduce.4
  987.8 20.5 all-reduce.6
where the time goes:
time: 1510 us
  local copies, waits for them, and re-layouts  571 us (38%)
  other arithmetic  551 us (36%)
  blocking collectives  215 us (14%)
  waiting for transfers between devices  93.6 us (6%)
  starting transfers between devices  51 us (3%)
  between operations  23.4 us (2%)
    scatter-add x12, other arithmetic, spread(): jax.ops.segment_sum(values, index, num_segments=total)  408 us
    gather x12, local copies, waits for them, and re-layouts, on_device(): changed = window[:, second] - rotate(rotation, direction[:, first])  197 us
    psum x4, blocking collectives, precond_sum(): return lax.psum(jnp.sum(residual * scaled), 'blk')  121 us
    unnamed x174, local copies, waits for them, and re-layouts  61.6 us
    psum x2, blocking collectives, on_device(): step_size = norm_now / lax.psum(jnp.sum(direction * image), 'blk')  60.4 us
    ppermute x36, waiting for transfers between devices, shifted(): return lax.ppermute(value, axis, pairs)  52.6 us
    ppermute x36, starting transfers between devices, shifted(): return lax.ppermute(value, axis, pairs)  51 us
    gather x2, local copies, waits for them, and re-layouts, on_device(): window[:, second] - rotate(rotation, estimate[:, first])  48.6 us
  transfers between devices with their start and end apart: 38, of which 21 were waited for; matrix products, arithmetic and copies ran while one was open for 18% of the time, Pallas kernels for 0%

commit v1 on v0

v1 whole, which is shorter than its diff:
```python
import functools

import jax
import jax.numpy as jnp
from jax import lax
from jax.experimental import pallas as pl
from jax.experimental.pallas import tpu as pltpu
from jax.sharding import PartitionSpec as P

PASSES = 2
SOFTEN = 0.05
LANES = 128
SUB = 8
SPLITS = 2
BLOCK_ENTRIES = ((0, 0), (1, 1), (2, 2), (0, 1), (0, 2), (1, 2))
F32 = jnp.float32
BF16 = jnp.bfloat16


def rotation_entries(v):
    squared = v[0] * v[0] + v[1] * v[1] + v[2] * v[2]
    factor = 2.0 / (1.0 + squared)
    skewed = ((None, -v[2], v[1]), (v[2], None, -v[0]), (-v[1], v[0], None))
    rows = []
    for a in range(3):
        row = []
        for b in range(3):
            if a == b:
                row.append(1.0 + factor * (v[a] * v[a] - squared))
            else:
                row.append(factor * (skewed[a][b] + v[a] * v[b]))
        rows.append(row)
    return rows


def rotate(rows, y):
    return [rows[a][0] * y[0] + rows[a][1] * y[1] + rows[a][2] * y[2] for a in range(3)]


def rotate_back(rows, y):
    return [rows[0][a] * y[0] + rows[1][a] * y[1] + rows[2][a] * y[2] for a in range(3)]


class Sizes:
    def __init__(self, n_blk, n_rep, pairs, slots, cams):
        self.n_blk, self.n_rep = n_blk, n_rep
        self.pairs, self.slots, self.cams = pairs, slots, cams
        self.hi = cams // LANES
        self.tile_rows = 3 * self.hi
        self.chunks = slots // LANES
        assert pairs == SUB and slots % LANES == 0 and cams % (LANES * SUB) == 0 and n_blk % 2 == 0


def block_at(sz, row, c):
    return pl.ds((row * sz.chunks + c) * SUB, SUB)


def chunk(sz, ref, row, c):
    return ref[block_at(sz, row, c), :]


def gather3(sz, source, index):
    hi = lax.shift_right_logical(index, 7)
    lo = lax.bitwise_and(index, LANES - 1)
    out = [None] * 3
    for r in range(sz.hi):
        mask = hi == r
        for c in range(3):
            got = jnp.take_along_axis(source(c, r), lo, axis=1, mode="promise_in_bounds")
            out[c] = got if r == 0 else jnp.where(mask, got, out[c])
    return out


def far_source(sz, far):
    return lambda c, r: far[pl.ds((c * sz.hi + r) * SUB, SUB), :]


def own_source(sz, own):
    return lambda c, r: jnp.broadcast_to(own[pl.ds(c * sz.hi + r, 1), :], (SUB, LANES))


def build_far(sz, far, tile_at, b, sign):
    for k in range(sz.pairs):
        t = lax.rem(b + (sign * k + sz.n_blk), sz.n_blk)
        far[pl.ds(k, sz.tile_rows, stride=SUB), :] = tile_at(k % 2, lax.div(t, 2))


def store_split(sz, vals, ch, c, value):
    high = value.astype(BF16).astype(F32)
    vals[block_at(sz, 2 * ch, c), :] = high
    vals[block_at(sz, 2 * ch + 1, c), :] = value - high


def scatter(sz, channels, vals, index_ref, index_row, lhs, rhs):
    lane_iota = lax.broadcasted_iota(jnp.int32, (LANES, LANES), 0)
    row_iota = lax.broadcasted_iota(jnp.int32, (sz.hi, LANES), 0)
    for c in range(sz.chunks):
        for k in range(sz.pairs):
            one = lambda ref, row: ref[pl.ds((row * sz.chunks + c) * SUB + k, 1), :]
            columns = pl.ds((c * sz.pairs + k) * LANES, LANES)
            index = one(index_ref, index_row).astype(jnp.int32)
            lo = lax.bitwise_and(index, LANES - 1)
            mask = row_iota == lax.shift_right_logical(index, 7)
            rhs[:, columns] = jnp.where(lane_iota == lo, 1.0, 0.0).astype(BF16)
            for part in range(SPLITS):
                for ch in range(channels):
                    block = jnp.where(mask, one(vals, 2 * ch + part), 0.0).astype(BF16)
                    lhs[pl.ds((part * channels + ch) * sz.hi, sz.hi), columns] = block
    rows = SPLITS * channels * sz.hi
    out = lax.dot_general(
        lhs[pl.ds(0, rows), :], rhs[...], (((1,), (1,)), ((), ())), preferred_element_type=F32
    )
    half = channels * sz.hi
    return out[:half] + out[half:]


MEAS, ROT, CONF, FIRST, SECOND = 0, 3, 6, 9, 10
CHANNELS = 11


def pack_kernel(sz, meas, rot, conf, first, second, counts, start, anchor, table, est, est_copies, anchor_out, *sends):
    for c in range(sz.chunks):
        lanes = pl.ds(c * LANES, LANES)
        slot = lax.broadcasted_iota(jnp.int32, (sz.pairs, LANES), 1) + c * LANES
        live = slot < counts[...]
        for i in range(3):
            table[block_at(sz, MEAS + i, c), :] = meas[i, :, lanes]
            table[block_at(sz, ROT + i, c), :] = rot[i, :, lanes]
            table[block_at(sz, CONF + i, c), :] = jnp.where(live, conf[i, :, lanes], 0.0)
        table[block_at(sz, FIRST, c), :] = first[:, lanes].astype(F32)
        table[block_at(sz, SECOND, c), :] = second[:, lanes].astype(F32)
    count = CHANNELS * sz.chunks
    for k in range(1, sz.pairs):
        sends[k - 1][...] = table[pl.ds(k, count, stride=SUB), :]
    for c in range(3):
        for r in range(sz.hi):
            est[pl.ds(c * sz.hi + r, 1), :] = start[pl.ds(c, 1), pl.ds(r * LANES, LANES)]
    for r in range(sz.hi):
        anchor_out[pl.ds(r, 1), :] = anchor[:, pl.ds(r * LANES, LANES)]
    for i in range(sz.n_blk // 2):
        est_copies[i] = est[...]


def step_factors(scal, n):
    total = scal[0]
    for i in range(1, n):
        total = total + scal[i]
    s = [jnp.sum(total[i : i + 1, :], axis=1, keepdims=True) for i in range(4)]
    alpha0 = s[0] / s[1]
    rz1 = alpha0 * alpha0 * s[2] - s[0]
    onward = 1.0 + rz1 / s[0]
    curve = onward * onward * s[1] - 2.0 * onward * alpha0 * s[2] + alpha0 * alpha0 * s[3]
    alpha1 = rz1 / curve
    return alpha0 + alpha1 * onward, -alpha1 * alpha0


def misfit_kernel(sz, first_pass, b_ref, *refs):
    refs = list(refs)
    take = lambda count: [refs.pop(0) for _ in range(count)]
    (table,) = take(1)
    recvs = take(sz.pairs - 1) if first_pass else take(1)
    est_a, est_b, own = take(3)
    if not first_pass:
        z_a, z_b, u_a, u_b, z, u, scal = take(7)
    if first_pass:
        (table_in,) = take(1)
    wc_out, wc_in, sums = take(3)
    if not first_pass:
        weights_ref, own_new = take(2)
    far, vals, lhs, rhs = refs
    b = b_ref[0]
    if first_pass:
        count = CHANNELS * sz.chunks
        table_in[pl.ds(0, count, stride=SUB), :] = table[pl.ds(0, count, stride=SUB), :]
        for k in range(1, sz.pairs):
            table_in[pl.ds(k, count, stride=SUB), :] = recvs[k - 1][...]
        est_ref = own

        def tile_at(parity, q):
            return (est_b if parity else est_a)[q]
    else:
        table_in = recvs[0]
        along_z, along_u = step_factors(scal, sz.n_blk * sz.n_rep)
        own_new[...] = own[...] + along_z * z[...] + along_u * u[...]
        est_ref = own_new

        def tile_at(parity, q):
            e, zz, uu = (est_b, z_b, u_b) if parity else (est_a, z_a, u_a)
            return e[q] + along_z * zz[q] + along_u * uu[q]

    total = None
    for incoming in (False, True):
        edges = table_in if incoming else table
        wc_ref = wc_in if incoming else wc_out
        build_far(sz, far, tile_at, b, -1 if incoming else 1)
        for c in range(sz.chunks):
            first = chunk(sz, edges, FIRST, c).astype(jnp.int32)
            second = chunk(sz, edges, SECOND, c).astype(jnp.int32)
            rows = rotation_entries([chunk(sz, edges, ROT + i, c) for i in range(3)])
            if incoming:
                at_first = gather3(sz, far_source(sz, far), first)
                at_second = gather3(sz, own_source(sz, est_ref), second)
            else:
                at_first = gather3(sz, own_source(sz, est_ref), first)
                at_second = gather3(sz, far_source(sz, far), second)
            turned = rotate(rows, at_first)
            misfit = [chunk(sz, edges, MEAS + i, c) - (at_second[i] - turned[i]) for i in range(3)]
            conf = [chunk(sz, edges, CONF + i, c) for i in range(3)]
            energy = conf[0] * misfit[0] * misfit[0] + conf[1] * misfit[1] * misfit[1] + conf[2] * misfit[2] * misfit[2]
            weight = 1.0 / jnp.sqrt(energy + SOFTEN * SOFTEN)
            if not first_pass and not incoming:
                weights_ref[:, pl.ds(c * LANES, LANES)] = jnp.where(conf[0] > 0.0, weight, 0.0)
            wc = [weight * conf[i] for i in range(3)]
            for i in range(3):
                wc_ref[block_at(sz, i, c), :] = wc[i]
            push = [wc[i] * misfit[i] for i in range(3)]
            if incoming:
                for i in range(3):
                    store_split(sz, vals, i, c, push[i])
                    store_split(sz, vals, 3 + i, c, wc[i])
            else:
                back = rotate_back(rows, push)
                for i in range(3):
                    store_split(sz, vals, i, c, -back[i])
                for n, (p, q) in enumerate(BLOCK_ENTRIES):
                    entry = sum(rows[i][p] * wc[i] * rows[i][q] for i in range(3))
                    store_split(sz, vals, 3 + n, c, entry)
        channels = 6 if incoming else 9
        part = scatter(sz, channels, vals, edges, SECOND if incoming else FIRST, lhs, rhs)
        if incoming:
            cut = 6 * sz.hi
            sums[pl.ds(0, cut), :] = sums[pl.ds(0, cut), :] + part
        else:
            sums[...] = part


def apply_inverse(sz, inv, v):
    a00, a11, a22, a01, a02, a12 = inv
    return [
        a00 * v[0] + a01 * v[1] + a02 * v[2],
        a01 * v[0] + a11 * v[1] + a12 * v[2],
        a02 * v[0] + a12 * v[1] + a22 * v[2],
    ]


def comp(sz, ref, i):
    return ref[pl.ds(i * sz.hi, sz.hi), :]


def precond_kernel(sz, mine, other, est, anchor, residual, inverse, z, z_copies):
    total = mine[...] + other[...]
    part = lambda i: total[i * sz.hi : (i + 1) * sz.hi]
    anc = anchor[...]
    res = [part(i) - anc * comp(sz, est, i) for i in range(3)]
    p00, p11, p22 = [part(3 + i) + anc for i in range(3)]
    p01, p02, p12 = [part(6 + i) for i in range(3)]
    adj00 = p11 * p22 - p12 * p12
    adj01 = p02 * p12 - p01 * p22
    adj02 = p01 * p12 - p02 * p11
    adj11 = p00 * p22 - p02 * p02
    adj12 = p01 * p02 - p00 * p12
    adj22 = p00 * p11 - p01 * p01
    det = p00 * adj00 + p01 * adj01 + p02 * adj02
    inv = [a / det for a in (adj00, adj11, adj22, adj01, adj02, adj12)]
    scaled = apply_inverse(sz, inv, res)
    for i in range(3):
        residual[pl.ds(i * sz.hi, sz.hi), :] = res[i]
        z[pl.ds(i * sz.hi, sz.hi), :] = scaled[i]
    for i in range(6):
        inverse[pl.ds(i * sz.hi, sz.hi), :] = inv[i]
    for i in range(sz.n_blk // 2):
        z_copies[i] = z[...]


def image_kernel(sz, b_ref, table, table_in, wc_out, wc_in, z_a, z_b, z, sums, far, vals, lhs, rhs):
    b = b_ref[0]

    def tile_at(parity, q):
        return (z_b if parity else z_a)[q]

    for incoming in (False, True):
        edges = table_in if incoming else table
        wc_ref = wc_in if incoming else wc_out
        build_far(sz, far, tile_at, b, -1 if incoming else 1)
        for c in range(sz.chunks):
            first = chunk(sz, edges, FIRST, c).astype(jnp.int32)
            second = chunk(sz, edges, SECOND, c).astype(jnp.int32)
            rows = rotation_entries([chunk(sz, edges, ROT + i, c) for i in range(3)])
            if incoming:
                at_first = gather3(sz, far_source(sz, far), first)
                at_second = gather3(sz, own_source(sz, z), second)
            else:
                at_first = gather3(sz, own_source(sz, z), first)
                at_second = gather3(sz, far_source(sz, far), second)
            turned = rotate(rows, at_first)
            push = [chunk(sz, wc_ref, i, c) * (at_second[i] - turned[i]) for i in range(3)]
            if incoming:
                for i in range(3):
                    store_split(sz, vals, i, c, push[i])
            else:
                back = rotate_back(rows, push)
                for i in range(3):
                    store_split(sz, vals, i, c, -back[i])
        part = scatter(sz, 3, vals, edges, SECOND if incoming else FIRST, lhs, rhs)
        if incoming:
            sums[...] = sums[...] + part
        else:
            sums[...] = part


def second_precond_kernel(sz, mine, other, z, anchor, inverse, w, u, u_copies):
    total = mine[...] + other[...]
    anc = anchor[...]
    image = [total[i * sz.hi : (i + 1) * sz.hi] + anc * comp(sz, z, i) for i in range(3)]
    scaled = apply_inverse(sz, [comp(sz, inverse, i) for i in range(6)], image)
    for i in range(3):
        w[pl.ds(i * sz.hi, sz.hi), :] = image[i]
        u[pl.ds(i * sz.hi, sz.hi), :] = scaled[i]
    for i in range(sz.n_blk // 2):
        u_copies[i] = u[...]


def fold(value):
    rows = value.shape[0]
    out = value[:SUB]
    for i in range(1, rows // SUB):
        out = out + value[i * SUB : (i + 1) * SUB]
    return out


def products_kernel(sz, b_ref, table, wc_out, u_a, u_b, residual, z, w, u, anchor, scal, far):
    b = b_ref[0]

    def tile_at(parity, q):
        return (u_b if parity else u_a)[q]

    build_far(sz, far, tile_at, b, 1)
    acc = jnp.zeros((SUB, LANES), F32)
    for c in range(sz.chunks):
        first = chunk(sz, table, FIRST, c).astype(jnp.int32)
        second = chunk(sz, table, SECOND, c).astype(jnp.int32)
        rows = rotation_entries([chunk(sz, table, ROT + i, c) for i in range(3)])
        at_first = gather3(sz, own_source(sz, u), first)
        at_second = gather3(sz, far_source(sz, far), second)
        turned = rotate(rows, at_first)
        for i in range(3):
            gap = at_second[i] - turned[i]
            acc = acc + chunk(sz, wc_out, i, c) * gap * gap
    share = 1.0 / sz.n_rep
    res, zz, ww, uu = residual[...], z[...], w[...], u[...]
    s1 = fold(res * zz) * share
    s2 = fold(zz * ww) * share
    s3 = fold(ww * uu) * share
    anc = anchor[...]
    s4 = acc + share * fold(anc * (comp(sz, u, 0) * comp(sz, u, 0) + comp(sz, u, 1) * comp(sz, u, 1) + comp(sz, u, 2) * comp(sz, u, 2)))
    block = [jnp.sum(s, axis=0, keepdims=True) for s in (s1, s2, s3, s4)]
    block = jnp.concatenate(block + [jnp.zeros((SUB - 4, LANES), F32)], axis=0)
    for i in range(sz.n_blk * sz.n_rep):
        scal[i] = block


def final_kernel(sz, est, z, u, scal, out):
    along_z, along_u = step_factors(scal, sz.n_blk * sz.n_rep)
    new = est[...] + along_z * z[...] + along_u * u[...]
    for c in range(3):
        for r in range(sz.hi):
            row = c * sz.hi + r
            out[pl.ds(c, 1), pl.ds(r * LANES, LANES)] = new[row : row + 1]


def on_device(measured, rot_vector, confidence, first_local, second_local, edge_counts, start_angles, anchor):
    n_blk, n_rep = lax.axis_size("blk"), lax.axis_size("rep")
    sz = Sizes(n_blk, n_rep, first_local.shape[1], first_local.shape[2], start_angles.shape[1])
    half = n_blk // 2
    tile = (sz.tile_rows, LANES)
    f32 = lambda *shape: jax.ShapeDtypeStruct(shape, F32)
    b = lax.axis_index("blk").astype(jnp.int32).reshape(1)
    smem = pl.BlockSpec(memory_space=pltpu.SMEM)
    vmem = pl.BlockSpec(memory_space=pltpu.VMEM)
    wide = sz.pairs * sz.slots
    rows = sz.chunks * SUB

    def scratch(channels):
        return [
            pltpu.VMEM((sz.tile_rows * SUB, LANES), F32),
            pltpu.VMEM((channels * 2 * rows, LANES), F32),
            pltpu.VMEM((SPLITS * channels * sz.hi, wide), BF16),
            pltpu.VMEM((LANES, wide), BF16),
        ]

    def call(kernel, name, outs, args, scalars=0, scratch_shapes=()):
        return pl.pallas_call(
            kernel,
            name=name,
            out_shape=outs,
            in_specs=[smem] * scalars + [vmem] * (len(args) - scalars),
            out_specs=[vmem] * len(outs),
            scratch_shapes=list(scratch_shapes),
            compiler_params=pltpu.CompilerParams(vmem_limit_bytes=48 * 1024 * 1024),
        )(*args)

    groups = [[core + 2 * i for i in range(half)] for core in range(2)]
    swap = [(i, i ^ 1) for i in range(n_blk)]

    def all_tiles(copies):
        same = lax.all_to_all(copies, "blk", 0, 0, axis_index_groups=groups)
        return same, lax.ppermute(same, "blk", swap)

    def other_half(value):
        if n_rep == 2:
            return lax.ppermute(value, "rep", [(0, 1), (1, 0)])
        return lax.psum(value, "rep") - value

    def all_products(scal):
        return lax.all_to_all(scal, ("blk", "rep"), 0, 0)

    packed = call(
        functools.partial(pack_kernel, sz),
        "pack",
        [f32(CHANNELS * rows, LANES), f32(*tile), f32(half, *tile), f32(sz.hi, LANES)]
        + [f32(CHANNELS * sz.chunks, LANES)] * (sz.pairs - 1),
        [measured[:, 0], rot_vector[:, 0], confidence[:, 0], first_local[0], second_local[0], edge_counts[0], start_angles, anchor.reshape(1, -1)],
    )
    table, est, est_copies, anchor_rows = packed[:4]
    recvs = [
        lax.ppermute(packed[4 + k - 1], "blk", [(i, (i + k) % n_blk) for i in range(n_blk)])
        for k in range(1, sz.pairs)
    ]
    est_a, est_b = all_tiles(est_copies)

    wc_shape = f32(3 * rows, LANES)
    sums_shape = f32(9 * sz.hi, LANES)
    for sweep in range(PASSES):
        if sweep == 0:
            table_in, wc_out, wc_in, sums = call(
                functools.partial(misfit_kernel, sz, True),
                "misfit_first",
                [f32(CHANNELS * rows, LANES), wc_shape, wc_shape, sums_shape],
                [b, table, *recvs, est_a, est_b, est],
                1,
                scratch(9),
            )
        else:
            wc_out, wc_in, sums, weights, est = call(
                functools.partial(misfit_kernel, sz, False),
                "misfit_next",
                [wc_shape, wc_shape, sums_shape, f32(sz.pairs, sz.slots), f32(*tile)],
                [b, table, table_in, est_a, est_b, est, z_a, z_b, u_a, u_b, z, u, scal],
                1,
                scratch(9),
            )
        residual, inverse, z, z_copies = call(
            functools.partial(precond_kernel, sz),
            "precond",
            [f32(*tile), f32(6 * sz.hi, LANES), f32(*tile), f32(half, *tile)],
            [sums, other_half(sums), est, anchor_rows],
        )
        z_a, z_b = all_tiles(z_copies)
        (sums,) = call(
            functools.partial(image_kernel, sz),
            "image",
            [f32(*tile)],
            [b, table, table_in, wc_out, wc_in, z_a, z_b, z],
            1,
            scratch(3),
        )
        w, u, u_copies = call(
            functools.partial(second_precond_kernel, sz),
            "second_precond",
            [f32(*tile), f32(*tile), f32(half, *tile)],
            [sums, other_half(sums), z, anchor_rows, inverse],
        )
        u_a, u_b = all_tiles(u_copies)
        (scal,) = call(
            functools.partial(products_kernel, sz),
            "products",
            [f32(n_blk * n_rep, SUB, LANES)],
            [b, table, wc_out, u_a, u_b, residual, z, w, u, anchor_rows],
            1,
            [pltpu.VMEM((sz.tile_rows * SUB, LANES), F32)],
        )
        scal = all_products(scal)
    (estimate,) = call(functools.partial(final_kernel, sz), "final", [f32(3, sz.cams)], [est, z, u, scal])
    return (estimate, weights[None])


def solution(mesh):
    return jax.shard_map(
        on_device,
        mesh=mesh,
        in_specs=(
            P(None, "blk", None, "rep"),
            P(None, "blk", None, "rep"),
            P(None, "blk", None, "rep"),
            P("blk", None, "rep"),
            P("blk", None, "rep"),
            P("blk", None, "rep"),
            P(None, "blk"),
            P("blk"),
        ),
        out_specs=(P(None, "blk"), P("blk", None, "rep")),
        check_vma=False,
    )
```

time: 1510 us -> 139 us (0.09)
  local copies, waits for them, and re-layouts: 571 us -> 6.23 us
  other arithmetic: 551 us -> 0 us
  blocking collectives: 215 us -> 78.8 us
  waiting for transfers between devices: 93.6 us -> 28.3 us
  starting transfers between devices: 51 us -> 7.56 us
  between operations: 23.4 us -> 0.72 us
  Pallas kernels: 0 us -> 16.4 us
    scatter-add x12 -> x0, other arithmetic: 408 us -> none  [spread(): jax.ops.segment_sum(values, index, num_segments=total)]
    gather x18 -> x0, local copies, waits for them, and re-layouts: 288 us -> none  [the longest x12 197 us: on_device(): changed = window[:, second] - rotate(rotation, direction[:, first])]
    psum x10 -> x0, blocking collectives: 215 us -> none  [the longest x4 121 us: precond_sum(): return lax.psum(jnp.sum(residual * scaled), 'blk')]
    all_to_all x0 -> x7, blocking collectives: none -> 78.8 us  [the longest x5 57.4 us: all_tiles(): same = lax.all_to_all(copies, 'blk', 0, 0, axis_index_groups=groups)]
    slice x27 -> x0, local copies, waits for them, and re-layouts: 76.3 us -> none  [the longest x18 47.8 us: returned(): moved = shifted(current[:, half_width:width], 'blk', half_width)]
    unnamed x174 -> x16, local copies, waits for them, and re-layouts: 61.6 us -> 6.15 us
    ppermute x36 -> x16, starting transfers between devices: 51 us -> 7.56 us  [the longest x4 3.9 us: other_half(): return lax.ppermute(value, 'rep', [(0, 1), (1, 0)])]
    concatenate x11 -> x0, local copies, waits for them, and re-layouts: 41.5 us -> none  [the longest x3 16.4 us: window_of(): window = jnp.concatenate([window, ahead], axis=1)]
  transfers between devices with their start and end apart: 38 -> 16, of which waited for: 21 -> 12; matrix products, arithmetic and copies ran while one was open for 18% -> 0% of each run, Pallas kernels for 0% -> 0%
where the time goes in v1:
time: 139 us; the launch traced here: 138 us
  blocking collectives  78.8 us (57%)
  waiting for transfers between devices  28.3 us (20%)
  Pallas kernels  16.4 us (12%)
  starting transfers between devices  7.56 us (5%)
  local copies, waits for them, and re-layouts  6.23 us (4%)
    all_to_all x5, blocking collectives, all_tiles(): same = lax.all_to_all(copies, 'blk', 0, 0, axis_index_groups=groups)  57.4 us
    all_to_all x2, blocking collectives, all_products(): return lax.all_to_all(scal, ('blk', 'rep'), 0, 0)  21.4 us
    pallas_call x12, Pallas kernels, call(): pl.pallas_call(kernel, name=name, out_shape=outs, in_specs=[smem] * scala...  16.4 us
    ppermute x4, waiting for transfers between devices, other_half(): return lax.ppermute(value, 'rep', [(0, 1), (1, 0)])  12.6 us
    ppermute x7, waiting for transfers between devices, on_device(): lax.ppermute(packed[4 + k - 1], 'blk', [(i, (i + k) % n_blk) for i in ran...  9.9 us
    unnamed x16, local copies, waits for them, and re-layouts  6.15 us
    ppermute x5, waiting for transfers between devices, all_tiles(): return (same, lax.ppermute(same, 'blk', swap))  5.76 us
    ppermute x4, starting transfers between devices, other_half(): return lax.ppermute(value, 'rep', [(0, 1), (1, 0)])  3.9 us
  transfers between devices with their start and end apart: 16, of which 12 were waited for; matrix products, arithmetic and copies ran while one was open for 0% of the time, Pallas kernels for 0%

profile of v1, /device:TPU:0, one launch (start us, length us, event | category | flops | bytes accessed | tf_op | source)
XLA Modules:
  0.0 138.0 jit_solution(9030164195469668601)
XLA Ops:
  0.6 0.6 copy-done.7
  1.3 0.1 copy.10.counts
  1.4 0.6 copy-done.6
  2.0 0.9 copy-done
  2.9 0.9 copy-done.1
  3.8 0.9 copy-done.2
  4.6 0.8 copy-done.3
  5.4 0.7 copy-done.4
  6.1 0.7 copy-done.5
  6.9 0.1 pack.1
  7.0 15.0 %all_to_all.35.refs_8_.refs_2_ = f32[8,48,128]{2,1,0:T(8,128)S(1)} all-to-all(f32[8,48,128]{2,1,0:T(8,128)S(1)} %get-tuple-element.44), channel_id=1, replica_groups={{0,4,8,12,16,20,24,28},{2,6,10,14,18,22,26,30},{1,5,9,13,17,21,25,29},{..., dimensions={0} | all-to-all | bytes 393216 | tf_op jit(solution)/shard_map/all_to_all | solution.py:406
  22.0 0.0 collective-permute-start.7
  22.0 0.5 collective-permute-start
  22.5 1.1 collective-permute-start.1
  23.6 0.7 collective-permute-start.2
  24.3 0.3 collective-permute-start.3
  24.6 3.5 %collective-permute-done.refs_1_ = f32[66,128]{1,0:T(8,128)S(1)} collective-permute-done((f32[66,128]{1,0:T(8,128)S(1)}, f32[66,128]{1,0:T(8,128)S(1)}, u32[]{:S(2)}, u32[]{:S(2)}) %collective-permute-start) | collective-permute-done | bytes 33824 | tf_op jit(solution)/shard_map/ppermute | solution.py:426
  28.1 0.0 collective-permute-start.4
  28.1 1.5 %collective-permute-done.1.refs_2_ = f32[66,128]{1,0:T(8,128)S(1)} collective-permute-done((f32[66,128]{1,0:T(8,128)S(1)}, f32[66,128]{1,0:T(8,128)S(1)}, u32[]{:S(2)}, u32[]{:S(2)}) %collective-permute-start.1) | collective-permute-done | bytes 33824 | tf_op jit(solution)/shard_map/ppermute | solution.py:426
  29.6 0.0 collective-permute-done.2.refs_3_
  29.6 1.1 collective-permute-start.6
  30.6 3.7 %collective-permute-done.4.refs_5_ = f32[66,128]{1,0:T(8,128)S(1)} collective-permute-done((f32[66,128]{1,0:T(8,128)S(1)}, f32[66,128]{1,0:T(8,128)S(1)}, u32[]{:S(2)}, u32[]{:S(2)}) %collective-permute-start.4) | collective-permute-done | bytes 33824 | tf_op jit(solution)/shard_map/ppermute | solution.py:426
  34.4 1.2 collective-permute-done.5.refs_6_
  35.6 3.8 %misfit_first.1 = (f32[528,128]{1,0:T(8,128)S(1)}, f32[144,128]{1,0:T(8,128)S(1)}, f32[144,128]{1,0:T(8,128)S(1)}, f32[144,128]{1,0:T(8,128)S(1)}) custom-call(s32[1]{0:T(128)} %bitcast.b_ref, f32[528,128]{1,0:T(8,128)S(1)} %get-tuple-element.36.refs_0_.table, f32[66,128]{1,0:T(8,128)S(1)} %collective-permute-done.refs_1_, ...), custom_call_target="tpu_custom_call" | custom-call | tf_op jit(solution)/shard_map/misfit_first/pallas_call | solution.py:392
  39.4 1.6 %collective-permute-start.8 = (f32[144,128]{1,0:T(8,128)S(1)}, f32[144,128]{1,0:T(8,128)S(1)}, u32[]{:S(2)}, u32[]{:S(2)}) collective-permute-start(f32[144,128]{1,0:T(8,128)S(1)} %get-tuple-element.47.mine), channel_id=1, source_target_pairs={{0,1},{1,0},{2,3},{3,2},{4,5},{5,4},{6,7},{7,6},{8,9},{9,8},{10,11... | collective-permute-start | bytes 221192 | tf_op jit(solution)/shard_map/ppermute | solution.py:411
  40.9 2.9 %collective-permute-done.8.other = f32[144,128]{1,0:T(8,128)S(1)} collective-permute-done((f32[144,128]{1,0:T(8,128)S(1)}, f32[144,128]{1,0:T(8,128)S(1)}, u32[]{:S(2)}, u32[]{:S(2)}) %collective-permute-start.8) | collective-permute-done | bytes 73760 | tf_op jit(solution)/shard_map/ppermute | solution.py:411
  43.9 11.0 %all_to_all.36.z_a.refs_5_ = f32[8,48,128]{2,1,0:T(8,128)S(1)} all-to-all(f32[8,48,128]{2,1,0:T(8,128)S(1)} %get-tuple-element.49), channel_id=1, replica_groups={{0,4,8,12,16,20,24,28},{2,6,10,14,18,22,26,30},{1,5,9,13,17,21,25,29},{..., dimensions={0} | all-to-all | bytes 393216 | tf_op jit(solution)/shard_map/all_to_all | solution.py:406
  54.9 1.4 %collective-permute-done.9.z_b.refs_6_ = f32[8,48,128]{2,1,0:T(8,128)S(1)} collective-permute-done((f32[8,48,128]{2,1,0:T(8,128)S(1)}, f32[8,48,128]{2,1,0:T(8,128)S(1)}, u32[]{:S(2)}, u32[]{:S(2)}) %collective-permute-start.9) | collective-permute-done | bytes 196640 | tf_op jit(solution)/shard_map/ppermute | solution.py:407
  56.3 2.8 %image.2.mine = f32[48,128]{1,0:T(8,128)S(1)} custom-call(s32[1]{0:T(128)} %bitcast.b_ref, f32[528,128]{1,0:T(8,128)S(1)} %get-tuple-element.36.refs_0_.table, f32[528,128]{1,0:T(8,128)S(1)} %get-tuple-element.46.table_in.refs_1_, f32[144,128]{1,0:T(8,128)S(1)} %get-tuple-element.50.wc_out, f32[144,128]{1,0:T(8,128)S(1)} %get-tuple-element.51.wc_in, ...), custom_call_target="tpu_custom_call" | custom-call | tf_op jit(solution)/shard_map/image/pallas_call | solution.py:392
  59.1 1.5 %collective-permute-start.10 = (f32[48,128]{1,0:T(8,128)S(1)}, f32[48,128]{1,0:T(8,128)S(1)}, u32[]{:S(2)}, u32[]{:S(2)}) collective-permute-start(f32[48,128]{1,0:T(8,128)S(1)} %image.2.mine), channel_id=1, source_target_pairs={{0,1},{1,0},{2,3},{3,2},{4,5},{5,4},{6,7},{7,6},{8,9},{9,8},{10,11... | collective-permute-start | bytes 73736 | tf_op jit(solution)/shard_map/ppermute | solution.py:411
  60.7 2.3 %collective-permute-done.10.other = f32[48,128]{1,0:T(8,128)S(1)} collective-permute-done((f32[48,128]{1,0:T(8,128)S(1)}, f32[48,128]{1,0:T(8,128)S(1)}, u32[]{:S(2)}, u32[]{:S(2)}) %collective-permute-start.10) | collective-permute-done | bytes 24608 | tf_op jit(solution)/shard_map/ppermute | solution.py:411
  63.0 10.7 %all_to_all.37.u_a.refs_7_ = f32[8,48,128]{2,1,0:T(8,128)S(1)} all-to-all(f32[8,48,128]{2,1,0:T(8,128)S(1)} %get-tuple-element.54), channel_id=1, replica_groups={{0,4,8,12,16,20,24,28},{2,6,10,14,18,22,26,30},{1,5,9,13,17,21,25,29},{..., dimensions={0} | all-to-all | bytes 393216 | tf_op jit(solution)/shard_map/all_to_all | solution.py:406
  73.7 1.4 %collective-permute-done.11.u_b.refs_8_ = f32[8,48,128]{2,1,0:T(8,128)S(1)} collective-permute-done((f32[8,48,128]{2,1,0:T(8,128)S(1)}, f32[8,48,128]{2,1,0:T(8,128)S(1)}, u32[]{:S(2)}, u32[]{:S(2)}) %collective-permute-start.11) | collective-permute-done | bytes 196640 | tf_op jit(solution)/shard_map/ppermute | solution.py:407
  75.1 0.8 products.2
  75.9 11.1 %all_to_all.38.refs_11_ = f32[32,8,128]{2,1,0:T(8,128)S(1)} all-to-all(f32[32,8,128]{2,1,0:T(8,128)S(1)} %products.2), channel_id=1, replica_groups=mesh['blk'=16,'rep'=2] {'blk','rep'}, dimensions={0} | all-to-all | bytes 262144 | tf_op jit(solution)/shard_map/all_to_all | solution.py:415
  87.0 4.5 %misfit_next.1 = (f32[144,128]{1,0:T(8,128)S(1)}, f32[144,128]{1,0:T(8,128)S(1)}, f32[144,128]{1,0:T(8,128)S(1)}, f32[8,768]{1,0:T(8,128)}, f32[48,128]{1,0:T(8,128)S(1)}) custom-call(s32[1]{0:T(128)} %bitcast.b_ref, f32[528,128]{1,0:T(8,128)S(1)} %get-tuple-element.36.refs_0_.table, f32[528,128]{1,0:T(8,128)S(1)} %get-tuple-element.46.table_in.refs_1_, ...), custom_call_target="tpu_custom_call" | custom-call | tf_op jit(solution)/shard_map/misfit_next/pallas_call | solution.py:392
  91.4 0.3 collective-permute-start.12
  91.7 4.0 %collective-permute-done.12.other = f32[144,128]{1,0:T(8,128)S(1)} collective-permute-done((f32[144,128]{1,0:T(8,128)S(1)}, f32[144,128]{1,0:T(8,128)S(1)}, u32[]{:S(2)}, u32[]{:S(2)}) %collective-permute-start.12) | collective-permute-done | bytes 73760 | tf_op jit(solution)/shard_map/ppermute | solution.py:411
  95.8 10.2 %all_to_all.39.z_a = f32[8,48,128]{2,1,0:T(8,128)S(1)} all-to-all(f32[8,48,128]{2,1,0:T(8,128)S(1)} %get-tuple-element.63), channel_id=1, replica_groups={{0,4,8,12,16,20,24,28},{2,6,10,14,18,22,26,30},{1,5,9,13,17,21,25,29},{..., dimensions={0} | all-to-all | bytes 393216 | tf_op jit(solution)/shard_map/all_to_all | solution.py:406
  106.0 1.4 %collective-permute-done.13.z_b = f32[8,48,128]{2,1,0:T(8,128)S(1)} collective-permute-done((f32[8,48,128]{2,1,0:T(8,128)S(1)}, f32[8,48,128]{2,1,0:T(8,128)S(1)}, u32[]{:S(2)}, u32[]{:S(2)}) %collective-permute-start.13) | collective-permute-done | bytes 196640 | tf_op jit(solution)/shard_map/ppermute | solution.py:407
  107.5 2.8 %image.3.mine = f32[48,128]{1,0:T(8,128)S(1)} custom-call(s32[1]{0:T(128)} %bitcast.b_ref, f32[528,128]{1,0:T(8,128)S(1)} %get-tuple-element.36.refs_0_.table, f32[528,128]{1,0:T(8,128)S(1)} %get-tuple-element.46.table_in.refs_1_, f32[144,128]{1,0:T(8,128)S(1)} %get-tuple-element.61.wc_out, f32[144,128]{1,0:T(8,128)S(1)} %get-tuple-element.62.wc_in, ...), custom_call_target="tpu_custom_call" | custom-call | tf_op jit(solution)/shard_map/image/pallas_call | solution.py:392
  110.3 0.5 collective-permute-start.14
  110.7 3.4 %collective-permute-done.14.other = f32[48,128]{1,0:T(8,128)S(1)} collective-permute-done((f32[48,128]{1,0:T(8,128)S(1)}, f32[48,128]{1,0:T(8,128)S(1)}, u32[]{:S(2)}, u32[]{:S(2)}) %collective-permute-start.14) | collective-permute-done | bytes 24608 | tf_op jit(solution)/shard_map/ppermute | solution.py:411
  114.1 10.5 %all_to_all.40.u_a = f32[8,48,128]{2,1,0:T(8,128)S(1)} all-to-all(f32[8,48,128]{2,1,0:T(8,128)S(1)} %get-tuple-element.66), channel_id=1, replica_groups={{0,4,8,12,16,20,24,28},{2,6,10,14,18,22,26,30},{1,5,9,13,17,21,25,29},{..., dimensions={0} | all-to-all | bytes 393216 | tf_op jit(solution)/shard_map/all_to_all | solution.py:406
  124.6 1.4 %collective-permute-done.15.u_b = f32[8,48,128]{2,1,0:T(8,128)S(1)} collective-permute-done((f32[8,48,128]{2,1,0:T(8,128)S(1)}, f32[8,48,128]{2,1,0:T(8,128)S(1)}, u32[]{:S(2)}, u32[]{:S(2)}) %collective-permute-start.15) | collective-permute-done | bytes 196640 | tf_op jit(solution)/shard_map/ppermute | solution.py:407
  126.1 0.8 products.3
  126.9 10.3 %all_to_all.41.scal = f32[32,8,128]{2,1,0:T(8,128)S(1)} all-to-all(f32[32,8,128]{2,1,0:T(8,128)S(1)} %products.3), channel_id=1, replica_groups=mesh['blk'=16,'rep'=2] {'blk','rep'}, dimensions={0} | all-to-all | bytes 262144 | tf_op jit(solution)/shard_map/all_to_all | solution.py:415
  137.2 0.8 final.1
  (20 shorter events, 0.2 us)
Async XLA Ops:
  0.6 0.7 copy-start.7
  1.3 0.7 copy-start.6
  2.0 0.9 copy-start
  2.9 0.9 copy-start.1
  3.8 0.9 copy-start.2
  4.6 0.8 copy-start.3
  5.4 0.7 copy-start.4
  6.1 0.7 copy-start.5
  22.0 13.6 %collective-permute-start.7 = (f32[8,48,128]{2,1,0:T(8,128)S(1)}, f32[8,48,128]{2,1,0:T(8,128)S(1)}, u32[]{:S(2)}, u32[]{:S(2)}) collective-permute-start(f32[8,48,128]{2,1,0:T(8,128)S(1)} %all_to_all.35.refs_8_.refs_2_), channel_id=1, source_target_pairs={{0,2},{2,0},{4,6},{6,4},{8,10},{10,8},{12,14},{14,12},{16,18},{18,... | collective-permute-start | bytes 589832 | tf_op jit(solution)/shard_map/ppermute | solution.py:407
  22.0 6.1 %collective-permute-start = (f32[66,128]{1,0:T(8,128)S(1)}, f32[66,128]{1,0:T(8,128)S(1)}, u32[]{:S(2)}, u32[]{:S(2)}) collective-permute-start(f32[66,128]{1,0:T(8,128)S(1)} %get-tuple-element.37), channel_id=1, source_target_pairs={{0,2},{2,4},{4,6},{6,8},{8,10},{10,12},{12,14},{14,16},{16,18},{18... | collective-permute-start | bytes 101384 | tf_op jit(solution)/shard_map/ppermute | solution.py:426
  22.5 7.0 %collective-permute-start.1 = (f32[66,128]{1,0:T(8,128)S(1)}, f32[66,128]{1,0:T(8,128)S(1)}, u32[]{:S(2)}, u32[]{:S(2)}) collective-permute-start(f32[66,128]{1,0:T(8,128)S(1)} %get-tuple-element.38), channel_id=1, source_target_pairs={{0,4},{2,6},{4,8},{6,10},{8,12},{10,14},{12,16},{14,18},{16,20},{1... | collective-permute-start | bytes 101384 | tf_op jit(solution)/shard_map/ppermute | solution.py:426
  23.6 6.0 %collective-permute-start.2 = (f32[66,128]{1,0:T(8,128)S(1)}, f32[66,128]{1,0:T(8,128)S(1)}, u32[]{:S(2)}, u32[]{:S(2)}) collective-permute-start(f32[66,128]{1,0:T(8,128)S(1)} %get-tuple-element.39), channel_id=1, source_target_pairs={{0,6},{2,8},{4,10},{6,12},{8,14},{10,16},{12,18},{14,20},{16,22},{... | collective-permute-start | bytes 101384 | tf_op jit(solution)/shard_map/ppermute | solution.py:426
  24.3 6.3 %collective-permute-start.3 = (f32[66,128]{1,0:T(8,128)S(1)}, f32[66,128]{1,0:T(8,128)S(1)}, u32[]{:S(2)}, u32[]{:S(2)}) collective-permute-start(f32[66,128]{1,0:T(8,128)S(1)} %get-tuple-element.40), channel_id=1, source_target_pairs={{0,8},{2,10},{4,12},{6,14},{8,16},{10,18},{12,20},{14,22},{16,24},... | collective-permute-start | bytes 101384 | tf_op jit(solution)/shard_map/ppermute | solution.py:426
  28.1 6.3 %collective-permute-start.4 = (f32[66,128]{1,0:T(8,128)S(1)}, f32[66,128]{1,0:T(8,128)S(1)}, u32[]{:S(2)}, u32[]{:S(2)}) collective-permute-start(f32[66,128]{1,0:T(8,128)S(1)} %get-tuple-element.41), channel_id=1, source_target_pairs={{0,10},{2,12},{4,14},{6,16},{8,18},{10,20},{12,22},{14,24},{16,26}... | collective-permute-start | bytes 101384 | tf_op jit(solution)/shard_map/ppermute | solution.py:426
  29.6 6.0 %collective-permute-start.5 = (f32[66,128]{1,0:T(8,128)S(1)}, f32[66,128]{1,0:T(8,128)S(1)}, u32[]{:S(2)}, u32[]{:S(2)}) collective-permute-start(f32[66,128]{1,0:T(8,128)S(1)} %get-tuple-element.42), channel_id=1, source_target_pairs={{0,12},{2,14},{4,16},{6,18},{8,20},{10,22},{12,24},{14,26},{16,28}... | collective-permute-start | bytes 101384 | tf_op jit(solution)/shard_map/ppermute | solution.py:426
  29.6 6.0 %collective-permute-start.6 = (f32[66,128]{1,0:T(8,128)S(1)}, f32[66,128]{1,0:T(8,128)S(1)}, u32[]{:S(2)}, u32[]{:S(2)}) collective-permute-start(f32[66,128]{1,0:T(8,128)S(1)} %get-tuple-element.43), channel_id=1, source_target_pairs={{0,14},{2,16},{4,18},{6,20},{8,22},{10,24},{12,26},{14,28},{16,30}... | collective-permute-start | bytes 101384 | tf_op jit(solution)/shard_map/ppermute | solution.py:426
  39.4 4.5 %collective-permute-start.8 = (f32[144,128]{1,0:T(8,128)S(1)}, f32[144,128]{1,0:T(8,128)S(1)}, u32[]{:S(2)}, u32[]{:S(2)}) collective-permute-start(f32[144,128]{1,0:T(8,128)S(1)} %get-tuple-element.47.mine), channel_id=1, source_target_pairs={{0,1},{1,0},{2,3},{3,2},{4,5},{5,4},{6,7},{7,6},{8,9},{9,8},{10,11... | collective-permute-start | bytes 221192 | tf_op jit(solution)/shard_map/ppermute | solution.py:411
  54.9 1.4 %collective-permute-start.9 = (f32[8,48,128]{2,1,0:T(8,128)S(1)}, f32[8,48,128]{2,1,0:T(8,128)S(1)}, u32[]{:S(2)}, u32[]{:S(2)}) collective-permute-start(f32[8,48,128]{2,1,0:T(8,128)S(1)} %all_to_all.36.z_a.refs_5_), channel_id=1, source_target_pairs={{0,2},{2,0},{4,6},{6,4},{8,10},{10,8},{12,14},{14,12},{16,18},{18,... | collective-permute-start | bytes 589832 | tf_op jit(solution)/shard_map/ppermute | solution.py:407
  59.1 3.9 %collective-permute-start.10 = (f32[48,128]{1,0:T(8,128)S(1)}, f32[48,128]{1,0:T(8,128)S(1)}, u32[]{:S(2)}, u32[]{:S(2)}) collective-permute-start(f32[48,128]{1,0:T(8,128)S(1)} %image.2.mine), channel_id=1, source_target_pairs={{0,1},{1,0},{2,3},{3,2},{4,5},{5,4},{6,7},{7,6},{8,9},{9,8},{10,11... | collective-permute-start | bytes 73736 | tf_op jit(solution)/shard_map/ppermute | solution.py:411
  73.7 1.4 %collective-permute-start.11 = (f32[8,48,128]{2,1,0:T(8,128)S(1)}, f32[8,48,128]{2,1,0:T(8,128)S(1)}, u32[]{:S(2)}, u32[]{:S(2)}) collective-permute-start(f32[8,48,128]{2,1,0:T(8,128)S(1)} %all_to_all.37.u_a.refs_7_), channel_id=1, source_target_pairs={{0,2},{2,0},{4,6},{6,4},{8,10},{10,8},{12,14},{14,12},{16,18},{18,... | collective-permute-start | bytes 589832 | tf_op jit(solution)/shard_map/ppermute | solution.py:407
  91.4 4.4 %collective-permute-start.12 = (f32[144,128]{1,0:T(8,128)S(1)}, f32[144,128]{1,0:T(8,128)S(1)}, u32[]{:S(2)}, u32[]{:S(2)}) collective-permute-start(f32[144,128]{1,0:T(8,128)S(1)} %get-tuple-element.59.mine), channel_id=1, source_target_pairs={{0,1},{1,0},{2,3},{3,2},{4,5},{5,4},{6,7},{7,6},{8,9},{9,8},{10,11... | collective-permute-start | bytes 221192 | tf_op jit(solution)/shard_map/ppermute | solution.py:411
  106.0 1.4 %collective-permute-start.13 = (f32[8,48,128]{2,1,0:T(8,128)S(1)}, f32[8,48,128]{2,1,0:T(8,128)S(1)}, u32[]{:S(2)}, u32[]{:S(2)}) collective-permute-start(f32[8,48,128]{2,1,0:T(8,128)S(1)} %all_to_all.39.z_a), channel_id=1, source_target_pairs={{0,2},{2,0},{4,6},{6,4},{8,10},{10,8},{12,14},{14,12},{16,18},{18,... | collective-permute-start | bytes 589832 | tf_op jit(solution)/shard_map/ppermute | solution.py:407
  110.3 3.9 %collective-permute-start.14 = (f32[48,128]{1,0:T(8,128)S(1)}, f32[48,128]{1,0:T(8,128)S(1)}, u32[]{:S(2)}, u32[]{:S(2)}) collective-permute-start(f32[48,128]{1,0:T(8,128)S(1)} %image.3.mine), channel_id=1, source_target_pairs={{0,1},{1,0},{2,3},{3,2},{4,5},{5,4},{6,7},{7,6},{8,9},{9,8},{10,11... | collective-permute-start | bytes 73736 | tf_op jit(solution)/shard_map/ppermute | solution.py:411
  124.6 1.4 %collective-permute-start.15 = (f32[8,48,128]{2,1,0:T(8,128)S(1)}, f32[8,48,128]{2,1,0:T(8,128)S(1)}, u32[]{:S(2)}, u32[]{:S(2)}) collective-permute-start(f32[8,48,128]{2,1,0:T(8,128)S(1)} %all_to_all.40.u_a), channel_id=1, source_target_pairs={{0,2},{2,0},{4,6},{6,4},{8,10},{10,8},{12,14},{14,12},{16,18},{18,... | collective-permute-start | bytes 589832 | tf_op jit(solution)/shard_map/ppermute | solution.py:407

commit v2 on v1

v2 whole, which is shorter than its diff:
```python
import functools

import jax
import jax.numpy as jnp
from jax import lax
from jax.experimental import pallas as pl
from jax.experimental.pallas import tpu as pltpu
from jax.sharding import PartitionSpec as P

PASSES = 2
SOFTEN = 0.05
LANES = 128
SUB = 8
SPLITS = 2
BLOCK_ENTRIES = ((0, 0), (1, 1), (2, 2), (0, 1), (0, 2), (1, 2))
MEAS, ROT, CONF, FIRST, SECOND = 0, 3, 6, 9, 10
CHANNELS = 11
F32 = jnp.float32
BF16 = jnp.bfloat16


def rotation_entries(v):
    squared = v[0] * v[0] + v[1] * v[1] + v[2] * v[2]
    factor = 2.0 / (1.0 + squared)
    skewed = ((None, -v[2], v[1]), (v[2], None, -v[0]), (-v[1], v[0], None))
    rows = []
    for a in range(3):
        row = []
        for b in range(3):
            if a == b:
                row.append(1.0 + factor * (v[a] * v[a] - squared))
            else:
                row.append(factor * (skewed[a][b] + v[a] * v[b]))
        rows.append(row)
    return rows


def rotate(rows, y):
    return [rows[a][0] * y[0] + rows[a][1] * y[1] + rows[a][2] * y[2] for a in range(3)]


def rotate_back(rows, y):
    return [rows[0][a] * y[0] + rows[1][a] * y[1] + rows[2][a] * y[2] for a in range(3)]


class Sizes:
    def __init__(self, n_blk, n_rep, pairs, slots, cams):
        self.n_blk, self.n_rep = n_blk, n_rep
        self.pairs, self.slots, self.cams = pairs, slots, cams
        self.hi = cams // LANES
        self.tile_rows = 3 * self.hi
        self.chunks = slots // LANES
        self.edge_rows = CHANNELS * self.chunks
        assert pairs == SUB and slots % LANES == 0 and cams % (LANES * SUB) == 0 and n_blk % 2 == 0


def block_at(sz, row, c):
    return pl.ds((row * sz.chunks + c) * SUB, SUB)


def chunk(sz, ref, row, c):
    return ref[block_at(sz, row, c), :]


def gather3(sz, source, index):
    hi = lax.shift_right_logical(index, 7)
    lo = lax.bitwise_and(index, LANES - 1)
    out = [None] * 3
    for r in range(sz.hi):
        mask = hi == r
        for c in range(3):
            got = jnp.take_along_axis(source(c, r), lo, axis=1, mode="promise_in_bounds")
            out[c] = got if r == 0 else jnp.where(mask, got, out[c])
    return out


def far_source(sz, far):
    return lambda c, r: far[pl.ds((c * sz.hi + r) * SUB, SUB), :]


def own_source(sz, own):
    return lambda c, r: jnp.broadcast_to(own[pl.ds(c * sz.hi + r, 1), :], (SUB, LANES))


def build_far(sz, far, tile_at, b, sign):
    for k in range(sz.pairs):
        t = lax.rem(b + (sign * k + sz.n_blk), sz.n_blk)
        far[pl.ds(k, sz.tile_rows, stride=SUB), :] = tile_at(k % 2, lax.div(t, 2))


def store_split(sz, vals, ch, c, value):
    high = value.astype(BF16).astype(F32)
    vals[block_at(sz, 2 * ch, c), :] = high
    vals[block_at(sz, 2 * ch + 1, c), :] = value - high


def scatter(sz, channels, vals, index_ref, index_row, lhs, rhs):
    lane_iota = lax.broadcasted_iota(jnp.int32, (LANES, LANES), 0).astype(F32).astype(BF16)
    row_iota = lax.broadcasted_iota(jnp.int32, (sz.hi, LANES), 0).astype(F32).astype(BF16)
    one, zero = jnp.ones((), BF16), jnp.zeros((), BF16)
    for c in range(sz.chunks):
        index = chunk(sz, index_ref, index_row, c).astype(jnp.int32)
        lows = lax.bitwise_and(index, LANES - 1).astype(F32)
        highs = lax.shift_right_logical(index, 7).astype(F32)
        for k in range(sz.pairs):
            columns = pl.ds((c * sz.pairs + k) * LANES, LANES)
            lo = jnp.broadcast_to(lows[k : k + 1], (sz.hi, LANES)).astype(BF16)
            hi = jnp.broadcast_to(highs[k : k + 1], (sz.hi, LANES)).astype(BF16)
            for n in range(LANES // sz.hi):
                at = pl.ds(n * sz.hi, sz.hi)
                rhs[at, columns] = jnp.where(lane_iota[n * sz.hi : (n + 1) * sz.hi] == lo, one, zero)
            mask = row_iota == hi
            for part in range(SPLITS):
                for ch in range(channels):
                    row = vals[pl.ds(((2 * ch + part) * sz.chunks + c) * SUB + k, 1), :]
                    block = jnp.where(mask, jnp.broadcast_to(row, (sz.hi, LANES)).astype(BF16), zero)
                    lhs[pl.ds((part * channels + ch) * sz.hi, sz.hi), columns] = block
    rows = SPLITS * channels * sz.hi
    out = lax.dot_general(
        lhs[pl.ds(0, rows), :], rhs[...], (((1,), (1,)), ((), ())), preferred_element_type=F32
    )
    half = channels * sz.hi
    return out[:half] + out[half:]


def pack_kernel(sz, *refs):
    hbm, (table, est, anchor_out, send), local, sems = refs[:8], refs[8:12], refs[12:20], refs[20]
    copies = [pltpu.make_async_copy(src, dst, sems.at[i]) for i, (src, dst) in enumerate(zip(hbm, local))]
    for copy in copies:
        copy.start()
    for copy in copies:
        copy.wait()
    meas, rot, conf, first, second, counts, start, anchor = local
    b = lax.axis_index("blk")
    for c in range(sz.chunks):
        lanes = pl.ds(c * LANES, LANES)
        slot = lax.broadcasted_iota(jnp.int32, (sz.pairs, LANES), 1) + c * LANES
        live = slot < counts[...]
        for i in range(3):
            table[block_at(sz, MEAS + i, c), :] = meas[i, :, lanes]
            table[block_at(sz, ROT + i, c), :] = rot[i, :, lanes]
            table[block_at(sz, CONF + i, c), :] = jnp.where(live, conf[i, :, lanes], 0.0)
        table[block_at(sz, FIRST, c), :] = first[:, lanes].astype(F32)
        table[block_at(sz, SECOND, c), :] = second[:, lanes].astype(F32)
    for c in range(3):
        for r in range(sz.hi):
            est[pl.ds(c * sz.hi + r, 1), :] = start[pl.ds(c, 1), pl.ds(r * LANES, LANES)]
    for r in range(sz.hi):
        anchor_out[pl.ds(r, 1), :] = anchor[:, pl.ds(r * LANES, LANES)]
    parity = lax.rem(b, 2)
    count = sz.edge_rows
    for q in range(sz.n_blk // 2):
        for other in range(2):
            core = (1 - parity) if other else parity
            k = jnp.minimum(lax.rem(2 * q + core - b + sz.n_blk, sz.n_blk), sz.pairs - 1)
            at = count + sz.tile_rows if other else 0
            send[q, pl.ds(at, count), :] = table[pl.ds(k, count, stride=SUB), :]
        send[q, pl.ds(count, sz.tile_rows), :] = est[...]


def step_factors(scal, n):
    total = scal[0]
    for i in range(1, n):
        total = total + scal[i]
    s = [jnp.sum(total[i : i + 1, :], axis=1, keepdims=True) for i in range(4)]
    alpha0 = s[0] / s[1]
    rz1 = alpha0 * alpha0 * s[2] - s[0]
    onward = 1.0 + rz1 / s[0]
    curve = onward * onward * s[1] - 2.0 * onward * alpha0 * s[2] + alpha0 * alpha0 * s[3]
    alpha1 = rz1 / curve
    return alpha0 + alpha1 * onward, -alpha1 * alpha0


def gathered_change(sz, edges, far, own, incoming, c, rows):
    first = chunk(sz, edges, FIRST, c).astype(jnp.int32)
    second = chunk(sz, edges, SECOND, c).astype(jnp.int32)
    if incoming:
        at_first = gather3(sz, far_source(sz, far), first)
        at_second = gather3(sz, own_source(sz, own), second)
    else:
        at_first = gather3(sz, own_source(sz, own), first)
        at_second = gather3(sz, far_source(sz, far), second)
    turned = rotate(rows, at_first)
    return [at_second[i] - turned[i] for i in range(3)]


def edge_rotation(sz, edges, c):
    return rotation_entries([chunk(sz, edges, ROT + i, c) for i in range(3)])


def put3(sz, ref, c, values):
    for i in range(3):
        ref[block_at(sz, i, c), :] = values[i]


def get3(sz, ref, c):
    return [chunk(sz, ref, i, c) for i in range(3)]


def misfit_sums(sz, incoming, misfit_of, edges, wc_ref, weights_ref, sums, vals, lhs, rhs):
    for c in range(sz.chunks):
        rows = None
        if not incoming:
            rows = edge_rotation(sz, edges, c)
        misfit = misfit_of(c, rows)
        conf = [chunk(sz, edges, CONF + i, c) for i in range(3)]
        energy = conf[0] * misfit[0] * misfit[0] + conf[1] * misfit[1] * misfit[1] + conf[2] * misfit[2] * misfit[2]
        weight = 1.0 / jnp.sqrt(energy + SOFTEN * SOFTEN)
        if weights_ref is not None:
            weights_ref[:, pl.ds(c * LANES, LANES)] = jnp.where(conf[0] > 0.0, weight, 0.0)
        wc = [weight * conf[i] for i in range(3)]
        put3(sz, wc_ref, c, wc)
        push = [wc[i] * misfit[i] for i in range(3)]
        if incoming:
            for i in range(3):
                store_split(sz, vals, i, c, push[i])
                store_split(sz, vals, 3 + i, c, wc[i])
        else:
            back = rotate_back(rows, push)
            for i in range(3):
                store_split(sz, vals, i, c, -back[i])
            for n, (p, q) in enumerate(BLOCK_ENTRIES):
                entry = sum(rows[i][p] * wc[i] * rows[i][q] for i in range(3))
                store_split(sz, vals, 3 + n, c, entry)
    part = scatter(sz, 6 if incoming else 9, vals, edges, SECOND if incoming else FIRST, lhs, rhs)
    if incoming:
        cut = 6 * sz.hi
        sums[pl.ds(0, cut), :] = sums[pl.ds(0, cut), :] + part
    else:
        sums[...] = part


def first_misfit_kernel(sz, table, same, other, own, table_in, gap_out, gap_in, wc_out, wc_in, sums, far, vals, lhs, rhs):
    b = lax.axis_index("blk")
    count = sz.edge_rows
    table_in[pl.ds(0, count, stride=SUB), :] = table[pl.ds(0, count, stride=SUB), :]
    for k in range(1, sz.pairs):
        q = lax.div(lax.rem(b + (sz.n_blk - k), sz.n_blk), 2)
        if k % 2:
            block = other[q, pl.ds(count + sz.tile_rows, count), :]
        else:
            block = same[q, pl.ds(0, count), :]
        table_in[pl.ds(k, count, stride=SUB), :] = block

    def tile_at(parity, q):
        return (other if parity else same)[q, pl.ds(count, sz.tile_rows), :]

    for incoming in (False, True):
        edges, gap, wc_ref = (table_in, gap_in, wc_in) if incoming else (table, gap_out, wc_out)
        build_far(sz, far, tile_at, b, -1 if incoming else 1)

        def misfit_of(c, rows):
            rows = edge_rotation(sz, edges, c) if rows is None else rows
            change = gathered_change(sz, edges, far, own, incoming, c, rows)
            misfit = [chunk(sz, edges, MEAS + i, c) - change[i] for i in range(3)]
            put3(sz, gap, c, misfit)
            return misfit

        misfit_sums(sz, incoming, misfit_of, edges, wc_ref, None, sums, vals, lhs, rhs)


def next_misfit_kernel(
    sz, table, table_in, gap_out, gap_in, z_out, z_in, u_out, u_in, own, z, u, scal,
    wc_out, wc_in, sums, weights, own_new, vals, lhs, rhs,
):
    along_z, along_u = step_factors(scal, sz.n_blk * sz.n_rep)
    own_new[...] = own[...] + along_z * z[...] + along_u * u[...]
    for incoming in (False, True):
        edges, wc_ref = (table_in, wc_in) if incoming else (table, wc_out)
        old, by_z, by_u = (gap_in, z_in, u_in) if incoming else (gap_out, z_out, u_out)

        def misfit_of(c, rows):
            old3, z3, u3 = get3(sz, old, c), get3(sz, by_z, c), get3(sz, by_u, c)
            return [old3[i] - (along_z * z3[i] + along_u * u3[i]) for i in range(3)]

        misfit_sums(sz, incoming, misfit_of, edges, wc_ref, None if incoming else weights, sums, vals, lhs, rhs)


def apply_inverse(sz, inv, v):
    a00, a11, a22, a01, a02, a12 = inv
    return [
        a00 * v[0] + a01 * v[1] + a02 * v[2],
        a01 * v[0] + a11 * v[1] + a12 * v[2],
        a02 * v[0] + a12 * v[1] + a22 * v[2],
    ]


def comp(sz, ref, i):
    return ref[pl.ds(i * sz.hi, sz.hi), :]


def precond_kernel(sz, mine, other, est, anchor, residual, inverse, z, z_copies):
    total = mine[...] + other[...]
    part = lambda i: total[i * sz.hi : (i + 1) * sz.hi]
    anc = anchor[...]
    res = [part(i) - anc * comp(sz, est, i) for i in range(3)]
    p00, p11, p22 = [part(3 + i) + anc for i in range(3)]
    p01, p02, p12 = [part(6 + i) for i in range(3)]
    adj00 = p11 * p22 - p12 * p12
    adj01 = p02 * p12 - p01 * p22
    adj02 = p01 * p12 - p02 * p11
    adj11 = p00 * p22 - p02 * p02
    adj12 = p01 * p02 - p00 * p12
    adj22 = p00 * p11 - p01 * p01
    det = p00 * adj00 + p01 * adj01 + p02 * adj02
    inv = [a / det for a in (adj00, adj11, adj22, adj01, adj02, adj12)]
    scaled = apply_inverse(sz, inv, res)
    for i in range(3):
        residual[pl.ds(i * sz.hi, sz.hi), :] = res[i]
        z[pl.ds(i * sz.hi, sz.hi), :] = scaled[i]
    for i in range(6):
        inverse[pl.ds(i * sz.hi, sz.hi), :] = inv[i]
    for i in range(sz.n_blk // 2):
        z_copies[i] = z[...]


def image_kernel(sz, keep, table, table_in, wc_out, wc_in, z_a, z_b, z, sums, *refs):
    kept, (far, vals, lhs, rhs) = refs[:-4], refs[-4:]
    b = lax.axis_index("blk")

    def tile_at(parity, q):
        return (z_b if parity else z_a)[q]

    for incoming in (False, True):
        edges, wc_ref = (table_in, wc_in) if incoming else (table, wc_out)
        build_far(sz, far, tile_at, b, -1 if incoming else 1)
        for c in range(sz.chunks):
            rows = edge_rotation(sz, edges, c)
            change = gathered_change(sz, edges, far, z, incoming, c, rows)
            if keep:
                put3(sz, kept[int(incoming)], c, change)
            wc = get3(sz, wc_ref, c)
            push = [wc[i] * change[i] for i in range(3)]
            if incoming:
                for i in range(3):
                    store_split(sz, vals, i, c, push[i])
            else:
                back = rotate_back(rows, push)
                for i in range(3):
                    store_split(sz, vals, i, c, -back[i])
        part = scatter(sz, 3, vals, edges, SECOND if incoming else FIRST, lhs, rhs)
        if incoming:
            sums[...] = sums[...] + part
        else:
            sums[...] = part


def second_precond_kernel(sz, mine, other, z, anchor, inverse, w, u, u_copies):
    total = mine[...] + other[...]
    anc = anchor[...]
    image = [total[i * sz.hi : (i + 1) * sz.hi] + anc * comp(sz, z, i) for i in range(3)]
    scaled = apply_inverse(sz, [comp(sz, inverse, i) for i in range(6)], image)
    for i in range(3):
        w[pl.ds(i * sz.hi, sz.hi), :] = image[i]
        u[pl.ds(i * sz.hi, sz.hi), :] = scaled[i]
    for i in range(sz.n_blk // 2):
        u_copies[i] = u[...]


def fold(value):
    rows = value.shape[0]
    out = value[:SUB]
    for i in range(1, rows // SUB):
        out = out + value[i * SUB : (i + 1) * SUB]
    return out


def products_kernel(sz, keep, table, *refs):
    refs = list(refs)
    table_in = refs.pop(0) if keep else None
    wc_out, u_a, u_b, residual, z, w, u, anchor, scal = refs[:9]
    kept, far = refs[9:-1], refs[-1]
    b = lax.axis_index("blk")

    def tile_at(parity, q):
        return (u_b if parity else u_a)[q]

    acc = jnp.zeros((SUB, LANES), F32)
    for incoming in (False, True) if keep else (False,):
        edges = table_in if incoming else table
        build_far(sz, far, tile_at, b, -1 if incoming else 1)
        for c in range(sz.chunks):
            change = gathered_change(sz, edges, far, u, incoming, c, edge_rotation(sz, edges, c))
            if keep:
                put3(sz, kept[int(incoming)], c, change)
            if not incoming:
                wc = get3(sz, wc_out, c)
                for i in range(3):
                    acc = acc + wc[i] * change[i] * change[i]
    share = 1.0 / sz.n_rep
    res, zz, ww, uu = residual[...], z[...], w[...], u[...]
    s1 = fold(res * zz) * share
    s2 = fold(zz * ww) * share
    s3 = fold(ww * uu) * share
    anc = anchor[...]
    s4 = acc + share * fold(anc * (comp(sz, u, 0) * comp(sz, u, 0) + comp(sz, u, 1) * comp(sz, u, 1) + comp(sz, u, 2) * comp(sz, u, 2)))
    block = [jnp.sum(s, axis=0, keepdims=True) for s in (s1, s2, s3, s4)]
    block = jnp.concatenate(block + [jnp.zeros((SUB - 4, LANES), F32)], axis=0)
    for i in range(sz.n_blk * sz.n_rep):
        scal[i] = block


def final_kernel(sz, est, z, u, scal, out):
    along_z, along_u = step_factors(scal, sz.n_blk * sz.n_rep)
    new = est[...] + along_z * z[...] + along_u * u[...]
    for c in range(3):
        for r in range(sz.hi):
            row = c * sz.hi + r
            out[pl.ds(c, 1), pl.ds(r * LANES, LANES)] = new[row : row + 1]


def on_device(measured, rot_vector, confidence, first_local, second_local, edge_counts, start_angles, anchor):
    n_blk, n_rep = lax.axis_size("blk"), lax.axis_size("rep")
    sz = Sizes(n_blk, n_rep, first_local.shape[1], first_local.shape[2], start_angles.shape[1])
    half = n_blk // 2
    tile = (sz.tile_rows, LANES)
    f32 = lambda *shape: jax.ShapeDtypeStruct(shape, F32)
    vmem = pl.BlockSpec(memory_space=pltpu.VMEM)
    wide = sz.pairs * sz.slots
    rows = sz.chunks * SUB
    far_shape = pltpu.VMEM((sz.tile_rows * SUB, LANES), F32)

    def sums_scratch(channels):
        return [
            pltpu.VMEM((channels * 2 * rows, LANES), F32),
            pltpu.VMEM((SPLITS * channels * sz.hi, wide), BF16),
            pltpu.VMEM((LANES, wide), BF16),
        ]

    def call(kernel, name, outs, args, scratch_shapes=(), spec=vmem):
        return pl.pallas_call(
            kernel,
            name=name,
            out_shape=outs,
            in_specs=[spec] * len(args),
            out_specs=[vmem] * len(outs),
            scratch_shapes=list(scratch_shapes),
            compiler_params=pltpu.CompilerParams(vmem_limit_bytes=48 * 1024 * 1024),
        )(*args)

    groups = [[core + 2 * i for i in range(half)] for core in range(2)]
    swap = [(i, i ^ 1) for i in range(n_blk)]

    def all_tiles(copies):
        same = lax.all_to_all(copies, "blk", 0, 0, axis_index_groups=groups)
        return same, lax.ppermute(same, "blk", swap)

    def other_half(value):
        if n_rep == 2:
            return lax.ppermute(value, "rep", [(0, 1), (1, 0)])
        return lax.psum(value, "rep") - value

    def all_products(scal):
        return lax.all_to_all(scal, ("blk", "rep"), 0, 0)

    inputs = [
        measured[:, 0], rot_vector[:, 0], confidence[:, 0], first_local[0], second_local[0], edge_counts[0],
        start_angles, anchor.reshape(1, -1),
    ]
    table_shape = f32(CHANNELS * rows, LANES)
    table, est, anchor_rows, send = call(
        functools.partial(pack_kernel, sz),
        "pack",
        [table_shape, f32(*tile), f32(sz.hi, LANES), f32(half, 2 * sz.edge_rows + sz.tile_rows, LANES)],
        inputs,
        [pltpu.VMEM(x.shape, x.dtype) for x in inputs] + [pltpu.SemaphoreType.DMA((len(inputs),))],
        pl.BlockSpec(memory_space=pltpu.HBM),
    )
    same, other = all_tiles(send)

    per_edge = f32(3 * rows, LANES)
    sums_shape = f32(9 * sz.hi, LANES)
    for sweep in range(PASSES):
        last = sweep + 1 == PASSES
        if sweep == 0:
            table_in, gap_out, gap_in, wc_out, wc_in, sums = call(
                functools.partial(first_misfit_kernel, sz),
                "misfit_first",
                [table_shape, per_edge, per_edge, per_edge, per_edge, sums_shape],
                [table, same, other, est],
                [far_shape] + sums_scratch(9),
            )
        else:
            wc_out, wc_in, sums, weights, est = call(
                functools.partial(next_misfit_kernel, sz),
                "misfit_next",
                [per_edge, per_edge, sums_shape, f32(sz.pairs, sz.slots), f32(*tile)],
                [table, table_in, gap_out, gap_in, z_out, z_in, u_out, u_in, est, z, u, scal],
                sums_scratch(9),
            )
        residual, inverse, z, z_copies = call(
            functools.partial(precond_kernel, sz),
            "precond",
            [f32(*tile), f32(6 * sz.hi, LANES), f32(*tile), f32(half, *tile)],
            [sums, other_half(sums), est, anchor_rows],
        )
        z_a, z_b = all_tiles(z_copies)
        sums, *kept = call(
            functools.partial(image_kernel, sz, not last),
            "image",
            [f32(*tile)] + ([] if last else [per_edge, per_edge]),
            [table, table_in, wc_out, wc_in, z_a, z_b, z],
            [far_shape] + sums_scratch(3),
        )
        if not last:
            z_out, z_in = kept
        w, u, u_copies = call(
            functools.partial(second_precond_kernel, sz),
            "second_precond",
            [f32(*tile), f32(*tile), f32(half, *tile)],
            [sums, other_half(sums), z, anchor_rows, inverse],
        )
        u_a, u_b = all_tiles(u_copies)
        scal, *kept = call(
            functools.partial(products_kernel, sz, not last),
            "products",
            [f32(n_blk * n_rep, SUB, LANES)] + ([] if last else [per_edge, per_edge]),
            [table] + ([] if last else [table_in]) + [wc_out, u_a, u_b, residual, z, w, u, anchor_rows],
            [far_shape],
        )
        if not last:
            u_out, u_in = kept
        scal = all_products(scal)
    (estimate,) = call(functools.partial(final_kernel, sz), "final", [f32(3, sz.cams)], [est, z, u, scal])
    return (estimate, weights[None])


def solution(mesh):
    return jax.shard_map(
        on_device,
        mesh=mesh,
        in_specs=(
            P(None, "blk", None, "rep"),
            P(None, "blk", None, "rep"),
            P(None, "blk", None, "rep"),
            P("blk", None, "rep"),
            P("blk", None, "rep"),
            P("blk", None, "rep"),
            P(None, "blk"),
            P("blk"),
        ),
        out_specs=(P(None, "blk"), P("blk", None, "rep")),
        check_vma=False,
    )
```

time: 139 us -> 138 us (level)
  blocking collectives: 78.8 us -> 90.1 us
  waiting for transfers between devices: 28.3 us -> 20.5 us
  starting transfers between devices: 7.56 us -> 3.99 us
    all_to_all x5, blocking collectives: 57.4 us -> 68.6 us  [all_tiles(): same = lax.all_to_all(copies, 'blk', 0, 0, axis_index_groups=groups)]
    ppermute x7 -> x0, waiting for transfers between devices: 9.9 us -> none  [on_device(): lax.ppermute(packed[4 + k - 1], 'blk', [(i, (i + k) % n_blk) for i in ran...]
    ppermute x7 -> x0, starting transfers between devices: 3.64 us -> none  [on_device(): lax.ppermute(packed[4 + k - 1], 'blk', [(i, (i + k) % n_blk) for i in ran...]
    ppermute x5, waiting for transfers between devices: 5.76 us -> 7.96 us  [all_tiles(): return (same, lax.ppermute(same, 'blk', swap))]
  transfers between devices with their start and end apart: 16 -> 9, of which waited for: 12 -> 9; matrix products, arithmetic and copies ran while one was open for 0% -> 0% of each run, Pallas kernels for 0% -> 0%
where the time goes in v2:
time: 138 us; the launch traced here: 137 us
  blocking collectives  90.1 us (65%)
  waiting for transfers between devices  20.5 us (15%)
  Pallas kernels  15.3 us (11%)
  local copies, waits for them, and re-layouts  6.51 us (5%)
  starting transfers between devices  3.99 us (3%)
    all_to_all x5, blocking collectives, all_tiles(): same = lax.all_to_all(copies, 'blk', 0, 0, axis_index_groups=groups)  68.6 us
    all_to_all x2, blocking collectives, all_products(): return lax.all_to_all(scal, ('blk', 'rep'), 0, 0)  21.5 us
    pallas_call x12, Pallas kernels, call(): pl.pallas_call(kernel, name=name, out_shape=outs, in_specs=[spec] * len(a...  15.3 us
    ppermute x4, waiting for transfers between devices, other_half(): return lax.ppermute(value, 'rep', [(0, 1), (1, 0)])  12.6 us
    ppermute x5, waiting for transfers between devices, all_tiles(): return (same, lax.ppermute(same, 'blk', swap))  7.96 us
    unnamed x16, local copies, waits for them, and re-layouts  6.15 us
    ppermute x4, starting transfers between devices, other_half(): return lax.ppermute(value, 'rep', [(0, 1), (1, 0)])  3.91 us
  transfers between devices with their start and end apart: 9, of which 9 were waited for; matrix products, arithmetic and copies ran while one was open for 0% of the time, Pallas kernels for 0%

profile of v2, /device:TPU:0, one launch (start us, length us, event | category | flops | bytes accessed | tf_op | source)
XLA Modules:
  0.0 137.1 jit_solution(9861344914187837131)
XLA Ops:
  0.6 0.0 copy-start.7
  0.6 0.6 copy-done.7
  1.3 0.0 copy-start.6
  1.3 0.1 copy.11.refs_5_
  1.4 0.6 copy-done.6
  2.0 0.0 copy-start
  2.0 0.9 copy-done
  2.9 0.0 copy-start.1
  2.9 0.9 copy-done.1
  3.8 0.9 copy-done.2
  4.6 0.8 copy-done.3
  5.4 0.7 copy-done.4
  6.1 0.7 copy-done.5
  6.9 0.7 pack.1
  7.5 26.5 %all_to_all.35.same = f32[8,180,128]{2,1,0:T(8,128)S(1)} all-to-all(f32[8,180,128]{2,1,0:T(8,128)S(1)} %get-tuple-element.38), channel_id=1, replica_groups={{0,4,8,12,16,20,24,28},{2,6,10,14,18,22,26,30},{1,5,9,13,17,21,25,29},{..., dimensions={0} | all-to-all | bytes 1474560 | tf_op jit(solution)/shard_map/all_to_all | solution.py:445
  34.1 0.1 copy.12
  34.2 0.1 collective-permute-start
  34.3 2.2 %collective-permute-done = f32[8,180,128]{2,0,1:T(8,128)S(1)} collective-permute-done((f32[8,180,128]{2,0,1:T(8,128)S(1)}, f32[8,180,128]{2,0,1:T(8,128)S(1)}, u32[]{:S(2)}, u32[]{:S(2)}) %collective-permute-start) | collective-permute-done | bytes 737312 | tf_op jit(solution)/shard_map/ppermute | solution.py:446
  36.5 0.1 copy.13.other
  36.6 3.4 %misfit_first.1 = (f32[528,128]{1,0:T(8,128)S(1)}, f32[144,128]{1,0:T(8,128)S(1)}, f32[144,128]{1,0:T(8,128)S(1)}, f32[144,128]{1,0:T(8,128)S(1)}, f32[144,128]{1,0:T(8,128)S(1)}, /*index=5*/f32[144,128]{1,0:T(8,128)S(1)}) custom-call(f32[528,128]{1,0:T(8,128)S(1)} %get-tuple-element.37.table, f32[8,180,128]{2,1,0:T(8,128)S(1)} %all_to_all.35.same, ...), custom_call_target="tpu_custom_call" | custom-call | tf_op jit(solution)/shard_map/misfit_first/pallas_call | solution.py:431
  40.0 1.6 %collective-permute-start.1 = (f32[144,128]{1,0:T(8,128)S(1)}, f32[144,128]{1,0:T(8,128)S(1)}, u32[]{:S(2)}, u32[]{:S(2)}) collective-permute-start(f32[144,128]{1,0:T(8,128)S(1)} %get-tuple-element.45.mine), channel_id=1, source_target_pairs={{0,1},{1,0},{2,3},{3,2},{4,5},{5,4},{6,7},{7,6},{8,9},{9,8},{10,11... | collective-permute-start | bytes 221192 | tf_op jit(solution)/shard_map/ppermute | solution.py:450
  41.6 2.8 %collective-permute-done.1.other = f32[144,128]{1,0:T(8,128)S(1)} collective-permute-done((f32[144,128]{1,0:T(8,128)S(1)}, f32[144,128]{1,0:T(8,128)S(1)}, u32[]{:S(2)}, u32[]{:S(2)}) %collective-permute-start.1) | collective-permute-done | bytes 73760 | tf_op jit(solution)/shard_map/ppermute | solution.py:450
  44.5 11.2 %all_to_all.36.z_a = f32[8,48,128]{2,1,0:T(8,128)S(1)} all-to-all(f32[8,48,128]{2,1,0:T(8,128)S(1)} %get-tuple-element.47), channel_id=1, replica_groups={{0,4,8,12,16,20,24,28},{2,6,10,14,18,22,26,30},{1,5,9,13,17,21,25,29},{..., dimensions={0} | all-to-all | bytes 393216 | tf_op jit(solution)/shard_map/all_to_all | solution.py:445
  55.7 0.0 collective-permute-start.2
  55.7 1.4 %collective-permute-done.2.z_b = f32[8,48,128]{2,1,0:T(8,128)S(1)} collective-permute-done((f32[8,48,128]{2,1,0:T(8,128)S(1)}, f32[8,48,128]{2,1,0:T(8,128)S(1)}, u32[]{:S(2)}, u32[]{:S(2)}) %collective-permute-start.2) | collective-permute-done | bytes 196640 | tf_op jit(solution)/shard_map/ppermute | solution.py:446
  57.1 2.3 %image.2 = (f32[48,128]{1,0:T(8,128)S(1)}, f32[144,128]{1,0:T(8,128)S(1)}, f32[144,128]{1,0:T(8,128)S(1)}) custom-call(f32[528,128]{1,0:T(8,128)S(1)} %get-tuple-element.37.table, f32[528,128]{1,0:T(8,128)S(1)} %get-tuple-element.40.table_in.refs_0_, f32[144,128]{1,0:T(8,128)S(1)} %get-tuple-element.43.wc_out.refs_1_, ...), custom_call_target="tpu_custom_call" | custom-call | tf_op jit(solution)/shard_map/image/pallas_call | solution.py:431
  59.5 1.6 %collective-permute-start.3 = (f32[48,128]{1,0:T(8,128)S(1)}, f32[48,128]{1,0:T(8,128)S(1)}, u32[]{:S(2)}, u32[]{:S(2)}) collective-permute-start(f32[48,128]{1,0:T(8,128)S(1)} %get-tuple-element.51.mine), channel_id=1, source_target_pairs={{0,1},{1,0},{2,3},{3,2},{4,5},{5,4},{6,7},{7,6},{8,9},{9,8},{10,11... | collective-permute-start | bytes 73736 | tf_op jit(solution)/shard_map/ppermute | solution.py:450
  61.0 2.3 %collective-permute-done.3.other = f32[48,128]{1,0:T(8,128)S(1)} collective-permute-done((f32[48,128]{1,0:T(8,128)S(1)}, f32[48,128]{1,0:T(8,128)S(1)}, u32[]{:S(2)}, u32[]{:S(2)}) %collective-permute-start.3) | collective-permute-done | bytes 24608 | tf_op jit(solution)/shard_map/ppermute | solution.py:450
  63.4 10.2 %all_to_all.37.refs_2_ = f32[8,48,128]{2,1,0:T(8,128)S(1)} all-to-all(f32[8,48,128]{2,1,0:T(8,128)S(1)} %get-tuple-element.53), channel_id=1, replica_groups={{0,4,8,12,16,20,24,28},{2,6,10,14,18,22,26,30},{1,5,9,13,17,21,25,29},{..., dimensions={0} | all-to-all | bytes 393216 | tf_op jit(solution)/shard_map/all_to_all | solution.py:445
  73.6 0.0 collective-permute-start.4
  73.6 1.4 %collective-permute-done.4.refs_3_ = f32[8,48,128]{2,1,0:T(8,128)S(1)} collective-permute-done((f32[8,48,128]{2,1,0:T(8,128)S(1)}, f32[8,48,128]{2,1,0:T(8,128)S(1)}, u32[]{:S(2)}, u32[]{:S(2)}) %collective-permute-start.4) | collective-permute-done | bytes 196640 | tf_op jit(solution)/shard_map/ppermute | solution.py:446
  75.0 1.4 %products.2 = (f32[32,8,128]{2,1,0:T(8,128)S(1)}, f32[144,128]{1,0:T(8,128)S(1)}, f32[144,128]{1,0:T(8,128)S(1)}) custom-call(f32[528,128]{1,0:T(8,128)S(1)} %get-tuple-element.37.table, f32[528,128]{1,0:T(8,128)S(1)} %get-tuple-element.40.table_in.refs_0_, f32[144,128]{1,0:T(8,128)S(1)} %get-tuple-element.43.wc_out.refs_1_, ...), custom_call_target="tpu_custom_call" | custom-call | tf_op jit(solution)/shard_map/products/pallas_call | solution.py:431
  76.4 11.2 %all_to_all.38.scal = f32[32,8,128]{2,1,0:T(8,128)S(1)} all-to-all(f32[32,8,128]{2,1,0:T(8,128)S(1)} %get-tuple-element.59), channel_id=1, replica_groups=mesh['blk'=16,'rep'=2] {'blk','rep'}, dimensions={0} | all-to-all | bytes 262144 | tf_op jit(solution)/shard_map/all_to_all | solution.py:454
  87.6 3.4 %misfit_next.1 = (f32[144,128]{1,0:T(8,128)S(1)}, f32[144,128]{1,0:T(8,128)S(1)}, f32[144,128]{1,0:T(8,128)S(1)}, f32[8,768]{1,0:T(8,128)}, f32[48,128]{1,0:T(8,128)S(1)}) custom-call(f32[528,128]{1,0:T(8,128)S(1)} %get-tuple-element.37.table, f32[528,128]{1,0:T(8,128)S(1)} %get-tuple-element.40.table_in.refs_0_, f32[144,128]{1,0:T(8,128)S(1)} %get-tuple-element.41.gap_out, ...), custom_call_target="tpu_custom_call" | custom-call | tf_op jit(solution)/shard_map/misfit_next/pallas_call | solution.py:431
  91.0 0.3 collective-permute-start.5
  91.3 4.0 %collective-permute-done.5.other = f32[144,128]{1,0:T(8,128)S(1)} collective-permute-done((f32[144,128]{1,0:T(8,128)S(1)}, f32[144,128]{1,0:T(8,128)S(1)}, u32[]{:S(2)}, u32[]{:S(2)}) %collective-permute-start.5) | collective-permute-done | bytes 73760 | tf_op jit(solution)/shard_map/ppermute | solution.py:450
  95.4 10.2 %all_to_all.39.z_a = f32[8,48,128]{2,1,0:T(8,128)S(1)} all-to-all(f32[8,48,128]{2,1,0:T(8,128)S(1)} %get-tuple-element.65), channel_id=1, replica_groups={{0,4,8,12,16,20,24,28},{2,6,10,14,18,22,26,30},{1,5,9,13,17,21,25,29},{..., dimensions={0} | all-to-all | bytes 393216 | tf_op jit(solution)/shard_map/all_to_all | solution.py:445
  105.6 0.0 collective-permute-start.6
  105.6 1.4 %collective-permute-done.6.z_b = f32[8,48,128]{2,1,0:T(8,128)S(1)} collective-permute-done((f32[8,48,128]{2,1,0:T(8,128)S(1)}, f32[8,48,128]{2,1,0:T(8,128)S(1)}, u32[]{:S(2)}, u32[]{:S(2)}) %collective-permute-start.6) | collective-permute-done | bytes 196640 | tf_op jit(solution)/shard_map/ppermute | solution.py:446
  107.0 2.4 %image.3.mine = f32[48,128]{1,0:T(8,128)S(1)} custom-call(f32[528,128]{1,0:T(8,128)S(1)} %get-tuple-element.37.table, f32[528,128]{1,0:T(8,128)S(1)} %get-tuple-element.40.table_in.refs_0_, f32[144,128]{1,0:T(8,128)S(1)} %get-tuple-element.63.wc_out.refs_0_, f32[144,128]{1,0:T(8,128)S(1)} %get-tuple-element.64.wc_in, f32[8,48,128]{2,1,0:T(8,128)S(1)} %all_to_all.39.z_a, ...), custom_call_target="tpu_custom_call" | custom-call | tf_op jit(solution)/shard_map/image/pallas_call | solution.py:431
  109.4 0.5 collective-permute-start.7
  109.9 3.4 %collective-permute-done.7.other = f32[48,128]{1,0:T(8,128)S(1)} collective-permute-done((f32[48,128]{1,0:T(8,128)S(1)}, f32[48,128]{1,0:T(8,128)S(1)}, u32[]{:S(2)}, u32[]{:S(2)}) %collective-permute-start.7) | collective-permute-done | bytes 24608 | tf_op jit(solution)/shard_map/ppermute | solution.py:450
  113.3 10.5 %all_to_all.40.refs_1_ = f32[8,48,128]{2,1,0:T(8,128)S(1)} all-to-all(f32[8,48,128]{2,1,0:T(8,128)S(1)} %get-tuple-element.68), channel_id=1, replica_groups={{0,4,8,12,16,20,24,28},{2,6,10,14,18,22,26,30},{1,5,9,13,17,21,25,29},{..., dimensions={0} | all-to-all | bytes 393216 | tf_op jit(solution)/shard_map/all_to_all | solution.py:445
  123.8 0.0 collective-permute-start.8
  123.8 1.4 %collective-permute-done.8.refs_2_ = f32[8,48,128]{2,1,0:T(8,128)S(1)} collective-permute-done((f32[8,48,128]{2,1,0:T(8,128)S(1)}, f32[8,48,128]{2,1,0:T(8,128)S(1)}, u32[]{:S(2)}, u32[]{:S(2)}) %collective-permute-start.8) | collective-permute-done | bytes 196640 | tf_op jit(solution)/shard_map/ppermute | solution.py:446
  125.2 0.8 products.3
  126.0 10.3 %all_to_all.41.scal = f32[32,8,128]{2,1,0:T(8,128)S(1)} all-to-all(f32[32,8,128]{2,1,0:T(8,128)S(1)} %products.3), channel_id=1, replica_groups=mesh['blk'=16,'rep'=2] {'blk','rep'}, dimensions={0} | all-to-all | bytes 262144 | tf_op jit(solution)/shard_map/all_to_all | solution.py:454
  136.3 0.8 final.1
  (8 shorter events, 0.1 us)
Async XLA Ops:
  0.6 0.7 copy-start.7
  1.3 0.7 copy-start.6
  2.0 0.9 copy-start
  2.9 0.9 copy-start.1
  3.8 0.9 copy-start.2
  4.6 0.8 copy-start.3
  5.4 0.7 copy-start.4
  6.1 0.7 copy-start.5
  34.2 2.3 %collective-permute-start = (f32[8,180,128]{2,0,1:T(8,128)S(1)}, f32[8,180,128]{2,0,1:T(8,128)S(1)}, u32[]{:S(2)}, u32[]{:S(2)}) collective-permute-start(f32[8,180,128]{2,0,1:T(8,128)S(1)} %copy.12), channel_id=1, source_target_pairs={{0,2},{2,0},{4,6},{6,4},{8,10},{10,8},{12,14},{14,12},{16,18},{18,... | collective-permute-start | bytes 2211848 | tf_op jit(solution)/shard_map/ppermute | solution.py:446
  40.0 4.4 %collective-permute-start.1 = (f32[144,128]{1,0:T(8,128)S(1)}, f32[144,128]{1,0:T(8,128)S(1)}, u32[]{:S(2)}, u32[]{:S(2)}) collective-permute-start(f32[144,128]{1,0:T(8,128)S(1)} %get-tuple-element.45.mine), channel_id=1, source_target_pairs={{0,1},{1,0},{2,3},{3,2},{4,5},{5,4},{6,7},{7,6},{8,9},{9,8},{10,11... | collective-permute-start | bytes 221192 | tf_op jit(solution)/shard_map/ppermute | solution.py:450
  55.7 1.4 %collective-permute-start.2 = (f32[8,48,128]{2,1,0:T(8,128)S(1)}, f32[8,48,128]{2,1,0:T(8,128)S(1)}, u32[]{:S(2)}, u32[]{:S(2)}) collective-permute-start(f32[8,48,128]{2,1,0:T(8,128)S(1)} %all_to_all.36.z_a), channel_id=1, source_target_pairs={{0,2},{2,0},{4,6},{6,4},{8,10},{10,8},{12,14},{14,12},{16,18},{18,... | collective-permute-start | bytes 589832 | tf_op jit(solution)/shard_map/ppermute | solution.py:446
  59.5 3.9 %collective-permute-start.3 = (f32[48,128]{1,0:T(8,128)S(1)}, f32[48,128]{1,0:T(8,128)S(1)}, u32[]{:S(2)}, u32[]{:S(2)}) collective-permute-start(f32[48,128]{1,0:T(8,128)S(1)} %get-tuple-element.51.mine), channel_id=1, source_target_pairs={{0,1},{1,0},{2,3},{3,2},{4,5},{5,4},{6,7},{7,6},{8,9},{9,8},{10,11... | collective-permute-start | bytes 73736 | tf_op jit(solution)/shard_map/ppermute | solution.py:450
  73.6 1.4 %collective-permute-start.4 = (f32[8,48,128]{2,1,0:T(8,128)S(1)}, f32[8,48,128]{2,1,0:T(8,128)S(1)}, u32[]{:S(2)}, u32[]{:S(2)}) collective-permute-start(f32[8,48,128]{2,1,0:T(8,128)S(1)} %all_to_all.37.refs_2_), channel_id=1, source_target_pairs={{0,2},{2,0},{4,6},{6,4},{8,10},{10,8},{12,14},{14,12},{16,18},{18,... | collective-permute-start | bytes 589832 | tf_op jit(solution)/shard_map/ppermute | solution.py:446
  91.0 4.4 %collective-permute-start.5 = (f32[144,128]{1,0:T(8,128)S(1)}, f32[144,128]{1,0:T(8,128)S(1)}, u32[]{:S(2)}, u32[]{:S(2)}) collective-permute-start(f32[144,128]{1,0:T(8,128)S(1)} %get-tuple-element.61.mine), channel_id=1, source_target_pairs={{0,1},{1,0},{2,3},{3,2},{4,5},{5,4},{6,7},{7,6},{8,9},{9,8},{10,11... | collective-permute-start | bytes 221192 | tf_op jit(solution)/shard_map/ppermute | solution.py:450
  105.6 1.4 %collective-permute-start.6 = (f32[8,48,128]{2,1,0:T(8,128)S(1)}, f32[8,48,128]{2,1,0:T(8,128)S(1)}, u32[]{:S(2)}, u32[]{:S(2)}) collective-permute-start(f32[8,48,128]{2,1,0:T(8,128)S(1)} %all_to_all.39.z_a), channel_id=1, source_target_pairs={{0,2},{2,0},{4,6},{6,4},{8,10},{10,8},{12,14},{14,12},{16,18},{18,... | collective-permute-start | bytes 589832 | tf_op jit(solution)/shard_map/ppermute | solution.py:446
  109.4 3.9 %collective-permute-start.7 = (f32[48,128]{1,0:T(8,128)S(1)}, f32[48,128]{1,0:T(8,128)S(1)}, u32[]{:S(2)}, u32[]{:S(2)}) collective-permute-start(f32[48,128]{1,0:T(8,128)S(1)} %image.3.mine), channel_id=1, source_target_pairs={{0,1},{1,0},{2,3},{3,2},{4,5},{5,4},{6,7},{7,6},{8,9},{9,8},{10,11... | collective-permute-start | bytes 73736 | tf_op jit(solution)/shard_map/ppermute | solution.py:450
  123.8 1.4 %collective-permute-start.8 = (f32[8,48,128]{2,1,0:T(8,128)S(1)}, f32[8,48,128]{2,1,0:T(8,128)S(1)}, u32[]{:S(2)}, u32[]{:S(2)}) collective-permute-start(f32[8,48,128]{2,1,0:T(8,128)S(1)} %all_to_all.40.refs_1_), channel_id=1, source_target_pairs={{0,2},{2,0},{4,6},{6,4},{8,10},{10,8},{12,14},{14,12},{16,18},{18,... | collective-permute-start | bytes 589832 | tf_op jit(solution)/shard_map/ppermute | solution.py:446

commit v3 on v2

--- a/solution.py
+++ b/solution.py
@@ -123,14 +123,15 @@
     return out[:half] + out[half:]
 
 
-def pack_kernel(sz, *refs):
-    hbm, (table, est, anchor_out, send), local, sems = refs[:8], refs[8:12], refs[12:20], refs[20]
-    copies = [pltpu.make_async_copy(src, dst, sems.at[i]) for i, (src, dst) in enumerate(zip(hbm, local))]
-    for copy in copies:
-        copy.start()
-    for copy in copies:
-        copy.wait()
-    meas, rot, conf, first, second, counts, start, anchor = local
+def tile_kernel(sz, start, est, est_copies):
+    for c in range(3):
+        for r in range(sz.hi):
+            est[pl.ds(c * sz.hi + r, 1), :] = start[pl.ds(c, 1), pl.ds(r * LANES, LANES)]
+    for i in range(sz.n_blk // 2):
+        est_copies[i] = est[...]
+
+
+def pack_kernel(sz, meas, rot, conf, first, second, counts, anchor, after, table, anchor_out, *sends):
     b = lax.axis_index("blk")
     for c in range(sz.chunks):
         lanes = pl.ds(c * LANES, LANES)
@@ -142,20 +143,31 @@
             table[block_at(sz, CONF + i, c), :] = jnp.where(live, conf[i, :, lanes], 0.0)
         table[block_at(sz, FIRST, c), :] = first[:, lanes].astype(F32)
         table[block_at(sz, SECOND, c), :] = second[:, lanes].astype(F32)
-    for c in range(3):
-        for r in range(sz.hi):
-            est[pl.ds(c * sz.hi + r, 1), :] = start[pl.ds(c, 1), pl.ds(r * LANES, LANES)]
     for r in range(sz.hi):
         anchor_out[pl.ds(r, 1), :] = anchor[:, pl.ds(r * LANES, LANES)]
-    parity = lax.rem(b, 2)
+    step = 1 - 2 * lax.rem(b, 2)
     count = sz.edge_rows
-    for q in range(sz.n_blk // 2):
-        for other in range(2):
-            core = (1 - parity) if other else parity
-            k = jnp.minimum(lax.rem(2 * q + core - b + sz.n_blk, sz.n_blk), sz.pairs - 1)
-            at = count + sz.tile_rows if other else 0
-            send[q, pl.ds(at, count), :] = table[pl.ds(k, count, stride=SUB), :]
-        send[q, pl.ds(count, sz.tile_rows), :] = est[...]
+    for m in range(1, sz.pairs // 2):
+        sends[m - 1][pl.ds(0, count), :] = table[pl.ds(2 * m, count, stride=SUB), :]
+        sends[m - 1][pl.ds(count, count), :] = table[pl.ds(2 * m + step, count, stride=SUB), :]
+    sends[-1][...] = table[pl.ds(sz.pairs - 1, count, stride=SUB), :]
+
+
+def relay_kernel(sz, table, *refs):
+    recvs, relay = refs[:-1], refs[-1]
+    even_core = lax.rem(lax.axis_index("blk"), 2) == 0
+    count = sz.edge_rows
+    steps = sz.pairs // 2
+    for j in range(steps):
+        if j == 0:
+            from_even = table[pl.ds(1, count, stride=SUB), :]
+        else:
+            from_even = recvs[j - 1][pl.ds(count, count), :]
+        if j + 1 < steps:
+            from_odd = recvs[j][pl.ds(count, count), :]
+        else:
+            from_odd = recvs[-1][...]
+        relay[pl.ds(j * count, count), :] = jnp.where(even_core, from_even, from_odd)
 
 
 def step_factors(scal, n):
@@ -230,33 +242,39 @@
         sums[...] = part
 
 
-def first_misfit_kernel(sz, table, same, other, own, table_in, gap_out, gap_in, wc_out, wc_in, sums, far, vals, lhs, rhs):
-    b = lax.axis_index("blk")
+def first_misfit(sz, incoming, edges, tile_at, own, gap, wc_ref, sums, far, vals, lhs, rhs):
+    build_far(sz, far, tile_at, lax.axis_index("blk"), -1 if incoming else 1)
+
+    def misfit_of(c, rows):
+        rows = edge_rotation(sz, edges, c) if rows is None else rows
+        change = gathered_change(sz, edges, far, own, incoming, c, rows)
+        misfit = [chunk(sz, edges, MEAS + i, c) - change[i] for i in range(3)]
+        put3(sz, gap, c, misfit)
+        return misfit
+
+    misfit_sums(sz, incoming, misfit_of, edges, wc_ref, None, sums, vals, lhs, rhs)
+
+
+def outgoing_misfit_kernel(sz, table, est_a, est_b, own, gap, wc, sums, *scratch):
+    tile_at = lambda parity, q: (est_b if parity else est_a)[q]
+    first_misfit(sz, False, table, tile_at, own, gap, wc, sums, *scratch)
+
+
+def incoming_misfit_kernel(sz, table, relayed, *refs):
+    steps = sz.pairs // 2
+    recvs, (est_a, est_b, own, sums_out, table_in, gap, wc, sums), scratch = refs[: steps - 1], refs[steps - 1 : -4], refs[-4:]
     count = sz.edge_rows
-    table_in[pl.ds(0, count, stride=SUB), :] = table[pl.ds(0, count, stride=SUB), :]
-    for k in range(1, sz.pairs):
-        q = lax.div(lax.rem(b + (sz.n_blk - k), sz.n_blk), 2)
-        if k % 2:
-            block = other[q, pl.ds(count + sz.tile_rows, count), :]
+    for k in range(sz.pairs):
+        if k == 0:
+            block = table[pl.ds(0, count, stride=SUB), :]
+        elif k % 2:
+            block = relayed[pl.ds((k // 2) * count, count), :]
         else:
-            block = same[q, pl.ds(0, count), :]
+            block = recvs[k // 2 - 1][pl.ds(0, count), :]
         table_in[pl.ds(k, count, stride=SUB), :] = block
-
-    def tile_at(parity, q):
-        return (other if parity else same)[q, pl.ds(count, sz.tile_rows), :]
-
-    for incoming in (False, True):
-        edges, gap, wc_ref = (table_in, gap_in, wc_in) if incoming else (table, gap_out, wc_out)
-        build_far(sz, far, tile_at, b, -1 if incoming else 1)
-
-        def misfit_of(c, rows):
-            rows = edge_rotation(sz, edges, c) if rows is None else rows
-            change = gathered_change(sz, edges, far, own, incoming, c, rows)
-            misfit = [chunk(sz, edges, MEAS + i, c) - change[i] for i in range(3)]
-            put3(sz, gap, c, misfit)
-            return misfit
-
-        misfit_sums(sz, incoming, misfit_of, edges, wc_ref, None, sums, vals, lhs, rhs)
+    sums[...] = sums_out[...]
+    tile_at = lambda parity, q: (est_b if parity else est_a)[q]
+    first_misfit(sz, True, table_in, tile_at, own, gap, wc, sums, *scratch)
 
 
 def next_misfit_kernel(
@@ -427,14 +445,15 @@
             pltpu.VMEM((LANES, wide), BF16),
         ]
 
-    def call(kernel, name, outs, args, scratch_shapes=(), spec=vmem):
+    def call(kernel, name, outs, args, scratch_shapes=()):
         return pl.pallas_call(
             kernel,
             name=name,
             out_shape=outs,
-            in_specs=[spec] * len(args),
+            in_specs=[vmem] * len(args),
             out_specs=[vmem] * len(outs),
             scratch_shapes=list(scratch_shapes),
+            cost_estimate=pl.CostEstimate(flops=20_000_000, bytes_accessed=1_000_000, transcendentals=0),
             compiler_params=pltpu.CompilerParams(vmem_limit_bytes=48 * 1024 * 1024),
         )(*args)
 
@@ -453,32 +472,46 @@
     def all_products(scal):
         return lax.all_to_all(scal, ("blk", "rep"), 0, 0)
 
-    inputs = [
-        measured[:, 0], rot_vector[:, 0], confidence[:, 0], first_local[0], second_local[0], edge_counts[0],
-        start_angles, anchor.reshape(1, -1),
-    ]
     table_shape = f32(CHANNELS * rows, LANES)
-    table, est, anchor_rows, send = call(
+    est, est_copies = call(functools.partial(tile_kernel, sz), "tile", [f32(*tile), f32(half, *tile)], [start_angles])
+    est_a, est_b = all_tiles(est_copies)
+    steps = sz.pairs // 2
+    table, anchor_rows, *sends = call(
         functools.partial(pack_kernel, sz),
         "pack",
-        [table_shape, f32(*tile), f32(sz.hi, LANES), f32(half, 2 * sz.edge_rows + sz.tile_rows, LANES)],
-        inputs,
-        [pltpu.VMEM(x.shape, x.dtype) for x in inputs] + [pltpu.SemaphoreType.DMA((len(inputs),))],
-        pl.BlockSpec(memory_space=pltpu.HBM),
+        [table_shape, f32(sz.hi, LANES)] + [f32(2 * sz.edge_rows, LANES)] * (steps - 1) + [f32(sz.edge_rows, LANES)],
+        [
+            measured[:, 0], rot_vector[:, 0], confidence[:, 0], first_local[0], second_local[0], edge_counts[0],
+            anchor.reshape(1, -1), est_b,
+        ],
     )
-    same, other = all_tiles(send)
+    recvs = [
+        lax.ppermute(sends[m - 1], "blk", [(i, (i + 2 * m) % n_blk) for i in range(n_blk)]) for m in range(1, steps)
+    ]
+    recvs.append(lax.ppermute(sends[-1], "blk", [(i, (i + sz.pairs) % n_blk) for i in range(1, n_blk, 2)]))
 
     per_edge = f32(3 * rows, LANES)
     sums_shape = f32(9 * sz.hi, LANES)
     for sweep in range(PASSES):
         last = sweep + 1 == PASSES
         if sweep == 0:
-            table_in, gap_out, gap_in, wc_out, wc_in, sums = call(
-                functools.partial(first_misfit_kernel, sz),
-                "misfit_first",
-                [table_shape, per_edge, per_edge, per_edge, per_edge, sums_shape],
-                [table, same, other, est],
+            gap_out, wc_out, sums = call(
+                functools.partial(outgoing_misfit_kernel, sz),
+                "misfit_outgoing",
+                [per_edge, per_edge, sums_shape],
+                [table, est_a, est_b, est],
                 [far_shape] + sums_scratch(9),
+            )
+            (relay,) = call(
+                functools.partial(relay_kernel, sz), "relay", [f32(steps * sz.edge_rows, LANES)], [table, *recvs]
+            )
+            relayed = lax.ppermute(relay, "blk", swap)
+            table_in, gap_in, wc_in, sums = call(
+                functools.partial(incoming_misfit_kernel, sz),
+                "misfit_incoming",
+                [table_shape, per_edge, per_edge, sums_shape],
+                [table, relayed, *recvs[:-1], est_a, est_b, est, sums],
+                [far_shape] + sums_scratch(6),
             )
         else:
             wc_out, wc_in, sums, weights, est = call(

time: 138 us -> 132 us (0.957)
  blocking collectives: 90.1 us -> 78.4 us
  waiting for transfers between devices: 20.5 us -> 27.8 us
  local copies, waits for them, and re-layouts: 6.51 us -> 1.52 us
  starting transfers between devices: 3.99 us -> 7.43 us
    all_to_all x5, blocking collectives: 68.6 us -> 57 us  [all_tiles(): same = lax.all_to_all(copies, 'blk', 0, 0, axis_index_groups=groups)]
    ppermute x0 -> x5, waiting for transfers between devices: none -> 8.48 us  [the longest x3 8.47 us: on_device(): lax.ppermute(sends[m - 1], 'blk', [(i, (i + 2 * m) % n_blk) for i in rang...]
    unnamed x16, local copies, waits for them, and re-layouts: 6.15 us -> 1.44 us
    ppermute x0 -> x5, starting transfers between devices: none -> 3.51 us  [the longest x3 2.79 us: on_device(): lax.ppermute(sends[m - 1], 'blk', [(i, (i + 2 * m) % n_blk) for i in rang...]
    ppermute x5, waiting for transfers between devices: 7.96 us -> 6.46 us  [all_tiles(): return (same, lax.ppermute(same, 'blk', swap))]
    pallas_call x12 -> x15, Pallas kernels: 15.3 us -> 15.3 us  [call(): pl.pallas_call(kernel, name=name, out_shape=outs, in_specs=[vmem] * len(a...]
  transfers between devices with their start and end apart: 9 -> 14, of which waited for: 9 -> 11; matrix products, arithmetic and copies ran while one was open for 0% -> 0% of each run, Pallas kernels for 0% -> 2%
where the time goes in v3:
time: 132 us; the launch traced here: 131 us
  blocking collectives  78.4 us (59%)
  waiting for transfers between devices  27.8 us (21%)
  Pallas kernels  15.3 us (12%)
  starting transfers between devices  7.43 us (6%)
  local copies, waits for them, and re-layouts  1.52 us (1%)
    all_to_all x5, blocking collectives, all_tiles(): same = lax.all_to_all(copies, 'blk', 0, 0, axis_index_groups=groups)  57 us
    all_to_all x2, blocking collectives, all_products(): return lax.all_to_all(scal, ('blk', 'rep'), 0, 0)  21.4 us
    pallas_call x15, Pallas kernels, call(): pl.pallas_call(kernel, name=name, out_shape=outs, in_specs=[vmem] * len(a...  15.3 us
    ppermute x4, waiting for transfers between devices, other_half(): return lax.ppermute(value, 'rep', [(0, 1), (1, 0)])  12.9 us
    ppermute x3, waiting for transfers between devices, on_device(): lax.ppermute(sends[m - 1], 'blk', [(i, (i + 2 * m) % n_blk) for i in rang...  8.47 us
    ppermute x5, waiting for transfers between devices, all_tiles(): return (same, lax.ppermute(same, 'blk', swap))  6.46 us
    ppermute x4, starting transfers between devices, other_half(): return lax.ppermute(value, 'rep', [(0, 1), (1, 0)])  3.91 us
    ppermute x3, starting transfers between devices, on_device(): lax.ppermute(sends[m - 1], 'blk', [(i, (i + 2 * m) % n_blk) for i in rang...  2.79 us
  transfers between devices with their start and end apart: 14, of which 11 were waited for; matrix products, arithmetic and copies ran while one was open for 0% of the time, Pallas kernels for 2%

profile of v3, /device:TPU:0, one launch (start us, length us, event | category | flops | bytes accessed | tf_op | source)
XLA Modules:
  0.0 131.3 jit_solution(17244451502817139270)
XLA Ops:
  0.6 0.7 copy-done.6
  1.4 0.0 copy-start
  1.4 0.0 copy-start.1
  1.4 0.0 copy-start.2
  1.5 0.0 copy-start.3
  1.5 0.0 copy-start.4
  1.5 15.2 %all_to_all.35.est_a.refs_3_ = f32[8,48,128]{2,1,0:T(8,128)S(1)} all-to-all(f32[8,48,128]{2,1,0:T(8,128)S(1)} %get-tuple-element.42), channel_id=1, replica_groups={{0,4,8,12,16,20,24,28},{2,6,10,14,18,22,26,30},{1,5,9,13,17,21,25,29},{..., dimensions={0} | all-to-all | bytes 393216 | tf_op jit(solution)/shard_map/all_to_all | solution.py:464
  16.6 0.0 collective-permute-start
  16.7 0.7 copy-done.7
  17.3 0.1 copy.10.counts
  17.4 0.7 collective-permute-done.after.est_b.refs_4_
  18.1 0.1 pack.1
  18.2 1.1 collective-permute-start.1
  19.4 0.3 collective-permute-start.2
  19.7 1.3 %collective-permute-start.3 = (f32[132,128]{1,0:T(8,128)S(1)}, f32[132,128]{1,0:T(8,128)S(1)}, u32[]{:S(2)}, u32[]{:S(2)}) collective-permute-start(f32[132,128]{1,0:T(8,128)S(1)} %get-tuple-element.46), channel_id=1, source_target_pairs={{0,12},{2,14},{4,16},{6,18},{8,20},{10,22},{12,24},{14,26},{16,28}... | collective-permute-start | bytes 202760 | tf_op jit(solution)/shard_map/ppermute | solution.py:489
  21.0 0.7 collective-permute-start.4
  21.7 0.0 collective-permute-done.4.refs_3_
  21.7 4.4 %collective-permute-done.1.refs_0_ = f32[132,128]{1,0:T(8,128)S(1)} collective-permute-done((f32[132,128]{1,0:T(8,128)S(1)}, f32[132,128]{1,0:T(8,128)S(1)}, u32[]{:S(2)}, u32[]{:S(2)}) %collective-permute-start.1) | collective-permute-done | bytes 67616 | tf_op jit(solution)/shard_map/ppermute | solution.py:489
  26.1 4.0 %collective-permute-done.3.refs_2_ = f32[132,128]{1,0:T(8,128)S(1)} collective-permute-done((f32[132,128]{1,0:T(8,128)S(1)}, f32[132,128]{1,0:T(8,128)S(1)}, u32[]{:S(2)}, u32[]{:S(2)}) %collective-permute-start.3) | collective-permute-done | bytes 67616 | tf_op jit(solution)/shard_map/ppermute | solution.py:489
  30.2 0.1 collective-permute-start.5
  30.3 2.1 %misfit_outgoing.1 = (f32[144,128]{1,0:T(8,128)S(1)}, f32[144,128]{1,0:T(8,128)S(1)}, f32[144,128]{1,0:T(8,128)S(1)}) custom-call(f32[528,128]{1,0:T(8,128)S(1)} %get-tuple-element.43.table, f32[8,48,128]{2,1,0:T(8,128)S(1)} %all_to_all.35.est_a.refs_3_, f32[8,48,128]{2,1,0:T(8,128)S(1)} %collective-permute-done.after.est_b.refs_4_, ...), custom_call_target="tpu_custom_call" | custom-call | flops 20000000 | bytes 1000000 | tf_op jit(solution)/shard_map/misfit_outgoing/pallas_call | solution.py:449
  32.4 0.0 collective-permute-done.5.relayed
  32.4 1.8 %misfit_incoming.1 = (f32[528,128]{1,0:T(8,128)S(1)}, f32[144,128]{1,0:T(8,128)S(1)}, f32[144,128]{1,0:T(8,128)S(1)}, f32[144,128]{1,0:T(8,128)S(1)}) custom-call(f32[528,128]{1,0:T(8,128)S(1)} %get-tuple-element.43.table, f32[264,128]{1,0:T(8,128)S(1)} %collective-permute-done.5.relayed, f32[132,128]{1,0:T(8,128)S(1)} %collective-permute-done.1.refs_0_, ...), custom_call_target="tpu_custom_call" | custom-call | flops 20000000 | bytes 1000000 | tf_op jit(solution)/shard_map/misfit_incoming/pallas_call | solution.py:449
  34.2 1.6 %collective-permute-start.6 = (f32[144,128]{1,0:T(8,128)S(1)}, f32[144,128]{1,0:T(8,128)S(1)}, u32[]{:S(2)}, u32[]{:S(2)}) collective-permute-start(f32[144,128]{1,0:T(8,128)S(1)} %get-tuple-element.55.mine), channel_id=1, source_target_pairs={{0,1},{1,0},{2,3},{3,2},{4,5},{5,4},{6,7},{7,6},{8,9},{9,8},{10,11... | collective-permute-start | bytes 221192 | tf_op jit(solution)/shard_map/ppermute | solution.py:469
  35.8 3.1 %collective-permute-done.6.other = f32[144,128]{1,0:T(8,128)S(1)} collective-permute-done((f32[144,128]{1,0:T(8,128)S(1)}, f32[144,128]{1,0:T(8,128)S(1)}, u32[]{:S(2)}, u32[]{:S(2)}) %collective-permute-start.6) | collective-permute-done | bytes 73760 | tf_op jit(solution)/shard_map/ppermute | solution.py:469
  38.9 10.4 %all_to_all.36.z_a = f32[8,48,128]{2,1,0:T(8,128)S(1)} all-to-all(f32[8,48,128]{2,1,0:T(8,128)S(1)} %get-tuple-element.57), channel_id=1, replica_groups={{0,4,8,12,16,20,24,28},{2,6,10,14,18,22,26,30},{1,5,9,13,17,21,25,29},{..., dimensions={0} | all-to-all | bytes 393216 | tf_op jit(solution)/shard_map/all_to_all | solution.py:464
  49.4 1.4 %collective-permute-done.7.z_b = f32[8,48,128]{2,1,0:T(8,128)S(1)} collective-permute-done((f32[8,48,128]{2,1,0:T(8,128)S(1)}, f32[8,48,128]{2,1,0:T(8,128)S(1)}, u32[]{:S(2)}, u32[]{:S(2)}) %collective-permute-start.7) | collective-permute-done | bytes 196640 | tf_op jit(solution)/shard_map/ppermute | solution.py:465
  50.8 2.4 %image.2 = (f32[48,128]{1,0:T(8,128)S(1)}, f32[144,128]{1,0:T(8,128)S(1)}, f32[144,128]{1,0:T(8,128)S(1)}) custom-call(f32[528,128]{1,0:T(8,128)S(1)} %get-tuple-element.43.table, f32[528,128]{1,0:T(8,128)S(1)} %get-tuple-element.50.table_in.refs_0_, f32[144,128]{1,0:T(8,128)S(1)} %get-tuple-element.53.wc_out.refs_1_, ...), custom_call_target="tpu_custom_call" | custom-call | flops 20000000 | bytes 1000000 | tf_op jit(solution)/shard_map/image/pallas_call | solution.py:449
  53.2 1.5 %collective-permute-start.8 = (f32[48,128]{1,0:T(8,128)S(1)}, f32[48,128]{1,0:T(8,128)S(1)}, u32[]{:S(2)}, u32[]{:S(2)}) collective-permute-start(f32[48,128]{1,0:T(8,128)S(1)} %get-tuple-element.61.mine), channel_id=1, source_target_pairs={{0,1},{1,0},{2,3},{3,2},{4,5},{5,4},{6,7},{7,6},{8,9},{9,8},{10,11... | collective-permute-start | bytes 73736 | tf_op jit(solution)/shard_map/ppermute | solution.py:469
  54.7 2.3 %collective-permute-done.8.other = f32[48,128]{1,0:T(8,128)S(1)} collective-permute-done((f32[48,128]{1,0:T(8,128)S(1)}, f32[48,128]{1,0:T(8,128)S(1)}, u32[]{:S(2)}, u32[]{:S(2)}) %collective-permute-start.8) | collective-permute-done | bytes 24608 | tf_op jit(solution)/shard_map/ppermute | solution.py:469
  57.1 10.7 %all_to_all.37.refs_2_ = f32[8,48,128]{2,1,0:T(8,128)S(1)} all-to-all(f32[8,48,128]{2,1,0:T(8,128)S(1)} %get-tuple-element.63), channel_id=1, replica_groups={{0,4,8,12,16,20,24,28},{2,6,10,14,18,22,26,30},{1,5,9,13,17,21,25,29},{..., dimensions={0} | all-to-all | bytes 393216 | tf_op jit(solution)/shard_map/all_to_all | solution.py:464
  67.8 0.0 collective-permute-start.9
  67.8 1.4 %collective-permute-done.9.refs_3_ = f32[8,48,128]{2,1,0:T(8,128)S(1)} collective-permute-done((f32[8,48,128]{2,1,0:T(8,128)S(1)}, f32[8,48,128]{2,1,0:T(8,128)S(1)}, u32[]{:S(2)}, u32[]{:S(2)}) %collective-permute-start.9) | collective-permute-done | bytes 196640 | tf_op jit(solution)/shard_map/ppermute | solution.py:465
  69.2 1.4 %products.2 = (f32[32,8,128]{2,1,0:T(8,128)S(1)}, f32[144,128]{1,0:T(8,128)S(1)}, f32[144,128]{1,0:T(8,128)S(1)}) custom-call(f32[528,128]{1,0:T(8,128)S(1)} %get-tuple-element.43.table, f32[528,128]{1,0:T(8,128)S(1)} %get-tuple-element.50.table_in.refs_0_, f32[144,128]{1,0:T(8,128)S(1)} %get-tuple-element.53.wc_out.refs_1_, ...), custom_call_target="tpu_custom_call" | custom-call | flops 20000000 | bytes 1000000 | tf_op jit(solution)/shard_map/products/pallas_call | solution.py:449
  70.6 11.1 %all_to_all.38.scal = f32[32,8,128]{2,1,0:T(8,128)S(1)} all-to-all(f32[32,8,128]{2,1,0:T(8,128)S(1)} %get-tuple-element.69), channel_id=1, replica_groups=mesh['blk'=16,'rep'=2] {'blk','rep'}, dimensions={0} | all-to-all | bytes 262144 | tf_op jit(solution)/shard_map/all_to_all | solution.py:473
  81.7 3.4 %misfit_next.1 = (f32[144,128]{1,0:T(8,128)S(1)}, f32[144,128]{1,0:T(8,128)S(1)}, f32[144,128]{1,0:T(8,128)S(1)}, f32[8,768]{1,0:T(8,128)}, f32[48,128]{1,0:T(8,128)S(1)}) custom-call(f32[528,128]{1,0:T(8,128)S(1)} %get-tuple-element.43.table, f32[528,128]{1,0:T(8,128)S(1)} %get-tuple-element.50.table_in.refs_0_, f32[144,128]{1,0:T(8,128)S(1)} %get-tuple-element.51.gap_out, ...), custom_call_target="tpu_custom_call" | custom-call | flops 20000000 | bytes 1000000 | tf_op jit(solution)/shard_map/misfit_next/pallas_call | solution.py:449
  85.2 0.3 collective-permute-start.10
  85.5 4.0 %collective-permute-done.10.other = f32[144,128]{1,0:T(8,128)S(1)} collective-permute-done((f32[144,128]{1,0:T(8,128)S(1)}, f32[144,128]{1,0:T(8,128)S(1)}, u32[]{:S(2)}, u32[]{:S(2)}) %collective-permute-start.10) | collective-permute-done | bytes 73760 | tf_op jit(solution)/shard_map/ppermute | solution.py:469
  89.6 10.2 %all_to_all.39.z_a = f32[8,48,128]{2,1,0:T(8,128)S(1)} all-to-all(f32[8,48,128]{2,1,0:T(8,128)S(1)} %get-tuple-element.75), channel_id=1, replica_groups={{0,4,8,12,16,20,24,28},{2,6,10,14,18,22,26,30},{1,5,9,13,17,21,25,29},{..., dimensions={0} | all-to-all | bytes 393216 | tf_op jit(solution)/shard_map/all_to_all | solution.py:464
  99.7 1.4 %collective-permute-done.11.z_b = f32[8,48,128]{2,1,0:T(8,128)S(1)} collective-permute-done((f32[8,48,128]{2,1,0:T(8,128)S(1)}, f32[8,48,128]{2,1,0:T(8,128)S(1)}, u32[]{:S(2)}, u32[]{:S(2)}) %collective-permute-start.11) | collective-permute-done | bytes 196640 | tf_op jit(solution)/shard_map/ppermute | solution.py:465
  101.2 2.4 %image.3.mine = f32[48,128]{1,0:T(8,128)S(1)} custom-call(f32[528,128]{1,0:T(8,128)S(1)} %get-tuple-element.43.table, f32[528,128]{1,0:T(8,128)S(1)} %get-tuple-element.50.table_in.refs_0_, f32[144,128]{1,0:T(8,128)S(1)} %get-tuple-element.73.wc_out.refs_0_, f32[144,128]{1,0:T(8,128)S(1)} %get-tuple-element.74.wc_in, f32[8,48,128]{2,1,0:T(8,128)S(1)} %all_to_all.39.z_a, ...), custom_call_target="tpu_custom_call" | custom-call | flops 20000000 | bytes 1000000 | tf_op jit(solution)/shard_map/image/pallas_call | solution.py:449
  103.6 0.5 collective-permute-start.12
  104.0 3.4 %collective-permute-done.12.other = f32[48,128]{1,0:T(8,128)S(1)} collective-permute-done((f32[48,128]{1,0:T(8,128)S(1)}, f32[48,128]{1,0:T(8,128)S(1)}, u32[]{:S(2)}, u32[]{:S(2)}) %collective-permute-start.12) | collective-permute-done | bytes 24608 | tf_op jit(solution)/shard_map/ppermute | solution.py:469
  107.5 10.5 %all_to_all.40.refs_1_ = f32[8,48,128]{2,1,0:T(8,128)S(1)} all-to-all(f32[8,48,128]{2,1,0:T(8,128)S(1)} %get-tuple-element.78), channel_id=1, replica_groups={{0,4,8,12,16,20,24,28},{2,6,10,14,18,22,26,30},{1,5,9,13,17,21,25,29},{..., dimensions={0} | all-to-all | bytes 393216 | tf_op jit(solution)/shard_map/all_to_all | solution.py:464
  118.0 1.4 %collective-permute-done.13.refs_2_ = f32[8,48,128]{2,1,0:T(8,128)S(1)} collective-permute-done((f32[8,48,128]{2,1,0:T(8,128)S(1)}, f32[8,48,128]{2,1,0:T(8,128)S(1)}, u32[]{:S(2)}, u32[]{:S(2)}) %collective-permute-start.13) | collective-permute-done | bytes 196640 | tf_op jit(solution)/shard_map/ppermute | solution.py:465
  119.4 0.8 products.3
  120.2 10.3 %all_to_all.41.scal = f32[32,8,128]{2,1,0:T(8,128)S(1)} all-to-all(f32[32,8,128]{2,1,0:T(8,128)S(1)} %products.3), channel_id=1, replica_groups=mesh['blk'=16,'rep'=2] {'blk','rep'}, dimensions={0} | all-to-all | bytes 262144 | tf_op jit(solution)/shard_map/all_to_all | solution.py:473
  130.5 0.8 final.1
  (19 shorter events, 0.2 us)
Async XLA Ops:
  0.6 0.8 copy-start.6
  1.4 16.7 %copy-start = (f32[3,1,8,768]{3,2,1,0:T(8,128)S(1)}, f32[3,1,8,768]{3,2,1,0:T(8,128)}, u32[]{:S(2)}) copy-start(f32[3,1,8,768]{3,2,1,0:T(8,128)} %param.8) | copy-start | bytes 221188
  1.4 16.7 %copy-start.1 = (f32[3,1,8,768]{3,2,1,0:T(8,128)S(1)}, f32[3,1,8,768]{3,2,1,0:T(8,128)}, u32[]{:S(2)}) copy-start(f32[3,1,8,768]{3,2,1,0:T(8,128)} %param.9) | copy-start | bytes 221188
  1.4 16.7 %copy-start.2 = (f32[3,1,8,768]{3,2,1,0:T(8,128)S(1)}, f32[3,1,8,768]{3,2,1,0:T(8,128)}, u32[]{:S(2)}) copy-start(f32[3,1,8,768]{3,2,1,0:T(8,128)} %param.10) | copy-start | bytes 221188
  1.5 16.6 %copy-start.3 = (s32[1,8,768]{2,1,0:T(8,128)S(1)}, s32[1,8,768]{2,1,0:T(8,128)}, u32[]{:S(2)}) copy-start(s32[1,8,768]{2,1,0:T(8,128)} %param.11) | copy-start | bytes 73732
  1.5 16.6 %copy-start.4 = (s32[1,8,768]{2,1,0:T(8,128)S(1)}, s32[1,8,768]{2,1,0:T(8,128)}, u32[]{:S(2)}) copy-start(s32[1,8,768]{2,1,0:T(8,128)} %param.12) | copy-start | bytes 73732
  16.6 0.7 copy-start.7
  16.6 1.4 %collective-permute-start = (f32[8,48,128]{2,1,0:T(8,128)S(1)}, f32[8,48,128]{2,1,0:T(8,128)S(1)}, u32[]{:S(2)}, u32[]{:S(2)}) collective-permute-start(f32[8,48,128]{2,1,0:T(8,128)S(1)} %all_to_all.35.est_a.refs_3_), channel_id=1, source_target_pairs={{0,2},{2,0},{4,6},{6,4},{8,10},{10,8},{12,14},{14,12},{16,18},{18,... | collective-permute-start | bytes 589832 | tf_op jit(solution)/shard_map/ppermute | solution.py:465
  17.3 0.8 copy-start.5
  18.2 7.9 %collective-permute-start.1 = (f32[132,128]{1,0:T(8,128)S(1)}, f32[132,128]{1,0:T(8,128)S(1)}, u32[]{:S(2)}, u32[]{:S(2)}) collective-permute-start(f32[132,128]{1,0:T(8,128)S(1)} %get-tuple-element.44), channel_id=1, source_target_pairs={{0,4},{2,6},{4,8},{6,10},{8,12},{10,14},{12,16},{14,18},{16,20},{1... | collective-permute-start | bytes 202760 | tf_op jit(solution)/shard_map/ppermute | solution.py:489
  19.4 6.8 %collective-permute-start.2 = (f32[132,128]{1,0:T(8,128)S(1)}, f32[132,128]{1,0:T(8,128)S(1)}, u32[]{:S(2)}, u32[]{:S(2)}) collective-permute-start(f32[132,128]{1,0:T(8,128)S(1)} %get-tuple-element.45), channel_id=1, source_target_pairs={{0,8},{2,10},{4,12},{6,14},{8,16},{10,18},{12,20},{14,22},{16,24},... | collective-permute-start | bytes 202760 | tf_op jit(solution)/shard_map/ppermute | solution.py:489
  19.7 10.5 %collective-permute-start.3 = (f32[132,128]{1,0:T(8,128)S(1)}, f32[132,128]{1,0:T(8,128)S(1)}, u32[]{:S(2)}, u32[]{:S(2)}) collective-permute-start(f32[132,128]{1,0:T(8,128)S(1)} %get-tuple-element.46), channel_id=1, source_target_pairs={{0,12},{2,14},{4,16},{6,18},{8,20},{10,22},{12,24},{14,26},{16,28}... | collective-permute-start | bytes 202760 | tf_op jit(solution)/shard_map/ppermute | solution.py:489
  21.0 0.7 collective-permute-start.4
  30.2 2.2 %collective-permute-start.5 = (f32[264,128]{1,0:T(8,128)S(1)}, f32[264,128]{1,0:T(8,128)S(1)}, u32[]{:S(2)}, u32[]{:S(2)}) collective-permute-start(f32[264,128]{1,0:T(8,128)S(1)} %relay.1), channel_id=1, source_target_pairs={{0,2},{2,0},{4,6},{6,4},{8,10},{10,8},{12,14},{14,12},{16,18},{18,... | collective-permute-start | bytes 405512 | tf_op jit(solution)/shard_map/ppermute | solution.py:508
  34.2 4.7 %collective-permute-start.6 = (f32[144,128]{1,0:T(8,128)S(1)}, f32[144,128]{1,0:T(8,128)S(1)}, u32[]{:S(2)}, u32[]{:S(2)}) collective-permute-start(f32[144,128]{1,0:T(8,128)S(1)} %get-tuple-element.55.mine), channel_id=1, source_target_pairs={{0,1},{1,0},{2,3},{3,2},{4,5},{5,4},{6,7},{7,6},{8,9},{9,8},{10,11... | collective-permute-start | bytes 221192 | tf_op jit(solution)/shard_map/ppermute | solution.py:469
  49.4 1.4 %collective-permute-start.7 = (f32[8,48,128]{2,1,0:T(8,128)S(1)}, f32[8,48,128]{2,1,0:T(8,128)S(1)}, u32[]{:S(2)}, u32[]{:S(2)}) collective-permute-start(f32[8,48,128]{2,1,0:T(8,128)S(1)} %all_to_all.36.z_a), channel_id=1, source_target_pairs={{0,2},{2,0},{4,6},{6,4},{8,10},{10,8},{12,14},{14,12},{16,18},{18,... | collective-permute-start | bytes 589832 | tf_op jit(solution)/shard_map/ppermute | solution.py:465
  53.2 3.9 %collective-permute-start.8 = (f32[48,128]{1,0:T(8,128)S(1)}, f32[48,128]{1,0:T(8,128)S(1)}, u32[]{:S(2)}, u32[]{:S(2)}) collective-permute-start(f32[48,128]{1,0:T(8,128)S(1)} %get-tuple-element.61.mine), channel_id=1, source_target_pairs={{0,1},{1,0},{2,3},{3,2},{4,5},{5,4},{6,7},{7,6},{8,9},{9,8},{10,11... | collective-permute-start | bytes 73736 | tf_op jit(solution)/shard_map/ppermute | solution.py:469
  67.8 1.4 %collective-permute-start.9 = (f32[8,48,128]{2,1,0:T(8,128)S(1)}, f32[8,48,128]{2,1,0:T(8,128)S(1)}, u32[]{:S(2)}, u32[]{:S(2)}) collective-permute-start(f32[8,48,128]{2,1,0:T(8,128)S(1)} %all_to_all.37.refs_2_), channel_id=1, source_target_pairs={{0,2},{2,0},{4,6},{6,4},{8,10},{10,8},{12,14},{14,12},{16,18},{18,... | collective-permute-start | bytes 589832 | tf_op jit(solution)/shard_map/ppermute | solution.py:465
  85.2 4.4 %collective-permute-start.10 = (f32[144,128]{1,0:T(8,128)S(1)}, f32[144,128]{1,0:T(8,128)S(1)}, u32[]{:S(2)}, u32[]{:S(2)}) collective-permute-start(f32[144,128]{1,0:T(8,128)S(1)} %get-tuple-element.71.mine), channel_id=1, source_target_pairs={{0,1},{1,0},{2,3},{3,2},{4,5},{5,4},{6,7},{7,6},{8,9},{9,8},{10,11... | collective-permute-start | bytes 221192 | tf_op jit(solution)/shard_map/ppermute | solution.py:469
  99.7 1.4 %collective-permute-start.11 = (f32[8,48,128]{2,1,0:T(8,128)S(1)}, f32[8,48,128]{2,1,0:T(8,128)S(1)}, u32[]{:S(2)}, u32[]{:S(2)}) collective-permute-start(f32[8,48,128]{2,1,0:T(8,128)S(1)} %all_to_all.39.z_a), channel_id=1, source_target_pairs={{0,2},{2,0},{4,6},{6,4},{8,10},{10,8},{12,14},{14,12},{16,18},{18,... | collective-permute-start | bytes 589832 | tf_op jit(solution)/shard_map/ppermute | solution.py:465
  103.6 3.9 %collective-permute-start.12 = (f32[48,128]{1,0:T(8,128)S(1)}, f32[48,128]{1,0:T(8,128)S(1)}, u32[]{:S(2)}, u32[]{:S(2)}) collective-permute-start(f32[48,128]{1,0:T(8,128)S(1)} %image.3.mine), channel_id=1, source_target_pairs={{0,1},{1,0},{2,3},{3,2},{4,5},{5,4},{6,7},{7,6},{8,9},{9,8},{10,11... | collective-permute-start | bytes 73736 | tf_op jit(solution)/shard_map/ppermute | solution.py:469
  117.9 1.4 %collective-permute-start.13 = (f32[8,48,128]{2,1,0:T(8,128)S(1)}, f32[8,48,128]{2,1,0:T(8,128)S(1)}, u32[]{:S(2)}, u32[]{:S(2)}) collective-permute-start(f32[8,48,128]{2,1,0:T(8,128)S(1)} %all_to_all.40.refs_1_), channel_id=1, source_target_pairs={{0,2},{2,0},{4,6},{6,4},{8,10},{10,8},{12,14},{14,12},{16,18},{18,... | collective-permute-start | bytes 589832 | tf_op jit(solution)/shard_map/ppermute | solution.py:465
